TPU v7x, 32 devices: a 4x4x1 block of a 4x4x8 slice. The times are simulated.
32 devices in a mesh: sys: 1 (over z), aux: 4 (over y), orb: 8 (over x, core).
Axes of the slice: x: 4, y: 4, z: 1, core: 2. Of those that a mesh axis runs over, the one named last changes fastest.
The devices are a block of a 4x4x8 slice.
Arguments:
- fit_tensor: float32 [1160, 240, 240], P(('sys', 'aux'), 'orb')
- occ_orbitals: float32 [240, 50], P('sys')
Outputs:
- output: float32 [240, 240], P(('sys', 'orb'), 'aux')
All inputs are finite; a program needn't handle non-finite values.
Results may differ from a plain program's by a relative error of at most 0.001.
Values are sent between devices in bfloat16 or wider.
A program may use at most 768 MiB of HBM per device.

v0:
```python
import jax
import jax.numpy as jnp
from jax import lax
from jax.sharding import PartitionSpec as P

PREC_MODE = lax.Precision.HIGHEST


def solution(mesh):
    n_orb = mesh.shape['orb']
    half_steps = n_orb // 2
    shift_perm = [(src, (src - 1) % n_orb) for src in range(n_orb)]

    def local_fock(fit_loc, orbitals):
        q_loc, row_blk, n_bf = fit_loc.shape
        n_occ = orbitals.shape[1]
        my_orb = lax.axis_index('orb')
        own_rows = lax.dynamic_slice_in_dim(orbitals, my_orb * row_blk, row_blk, 0)
        dens_rows = jnp.einsum('mi,si->ms', own_rows, orbitals, precision=PREC_MODE, preferred_element_type=jnp.float32)
        fit_flat = fit_loc.reshape(q_loc, row_blk * n_bf)
        coef_part = jnp.dot(fit_flat, dens_rows.reshape(row_blk * n_bf), precision=PREC_MODE, preferred_element_type=jnp.float32)
        aux_coef = lax.psum(coef_part, 'orb')
        coul_rows = jnp.dot(aux_coef, fit_flat, precision=PREC_MODE, preferred_element_type=jnp.float32).reshape(row_blk, n_bf)
        half_t = jnp.dot(fit_loc.reshape(q_loc * row_blk, n_bf), orbitals, precision=PREC_MODE, preferred_element_type=jnp.float32).reshape(q_loc, row_blk, n_occ)

        def exch_block(t_other):
            return jnp.einsum('qmi,qni->mn', half_t, t_other, precision=PREC_MODE, preferred_element_type=jnp.float32)

        blocks = jnp.zeros((row_blk, n_orb, row_blk), jnp.float32)
        blocks = lax.dynamic_update_slice(blocks, exch_block(half_t)[:, None, :], (0, my_orb, 0))

        def pass_step(pass_idx, loop_state):
            t_moving, acc_blocks = loop_state
            t_moving = lax.ppermute(t_moving, 'orb', shift_perm)
            col_blk = (my_orb + pass_idx) % n_orb
            acc_blocks = lax.dynamic_update_slice(acc_blocks, exch_block(t_moving)[:, None, :], (0, col_blk, 0))
            return t_moving, acc_blocks

        blocks = lax.fori_loop(1, half_steps + 1, pass_step, (half_t, blocks))[1]
        mirror_out = jnp.transpose(blocks, (1, 2, 0))
        mirror_in = lax.all_to_all(mirror_out, 'orb', 0, 0, tiled=True)
        mirror_rows = jnp.transpose(mirror_in, (1, 0, 2))
        col_dist = (jnp.arange(n_orb) - my_orb) % n_orb
        keep_own = (col_dist <= half_steps)[None, :, None]
        exch_rows = jnp.where(keep_own, blocks, mirror_rows).reshape(row_blk, n_bf)
        g_part = 2.0 * coul_rows - exch_rows
        return lax.psum_scatter(g_part, 'aux', scatter_dimension=1, tiled=True)

    spec_fit = P(('sys', 'aux'), 'orb', None)
    spec_orbitals = P('sys', None)
    spec_out = P(('sys', 'orb'), 'aux')
    return jax.shard_map(local_fock, mesh=mesh, in_specs=(spec_fit, spec_orbitals), out_specs=spec_out, check_vma=False)
```

profile of v0, /device:TPU:96, one launch (start us, length us, event | category | flops | bytes accessed | tf_op | source)
XLA Modules:
  0.0 265.2 jit_solution(12931238748474471331)
XLA Ops:
  0.0 0.0 copy-start
  0.0 0.8 copy-done
  0.8 11.4 %fusion.4 = f32[290,30,50]{0,2,1:T(8,128)S(1)} fusion(f32[290,30,240]{2,0,1:T(8,128)} %param.4, f32[240,50]{0,1:T(8,128)S(1)} %copy-done), kind=kOutput, calls=%fused_computation.9 | convolution fusion | flops 1252800000 | bytes 10140000 | tf_op jit(solution)/shard_map/dot_general | solution.py:24
  12.2 1.9 copy.19
  14.1 3.3 %copy.36 = f32[290,30,50]{0,1,2:T(8,128)} copy(f32[290,30,50]{0,1,2:T(8,128)} %copy.19) | data formatting | bytes 3480000
  17.4 4.6 %fusion.3 = f32[30,8,30]{2,0,1:T(8,128)S(1)} fusion(f32[30,8,30]{2,0,1:T(8,128)S(1)} %broadcast_in_dim.26, s32[]{:T(128)S(6)} %select_n.52, f32[290,30,50]{0,1,2:T(8,128)} %copy.19), kind=kOutput, calls=%fused_computation.6 | convolution fusion | flops 156600000 | bytes 4931588 | tf_op jit(solution)/shard_map/qmi,qni->mn/dot_general | solution.py:27
  22.0 142.3 %while.17 = (s32[]{:T(128)}, f32[290,30,50]{0,1,2:T(8,128)}, f32[30,8,30]{2,0,1:T(8,128)S(1)}, f32[290,30,50]{0,1,2:T(8,128)}, s32[]{:T(128)}, /*index=5*/s32[]{:T(128)}, s32[]{:T(128)}, s32[]{:T(128)}, s32[]{:T(128)}) while((s32[]{:T(128)}, f32[290,30,50]{0,1,2:T(8,128)}, f32[30,8,30]{2,0,1:T(8,128)S(1)}, f32[290,30,50]{0,1,2:T(8,128)}, ...), condition=%wide.region_2.3_spmd, body=%wide.region_1.2_spmd.sunk | while | flops 156600016 | bytes 14654276 | solution.py:39
  22.0 2.1 collective-permute-start
  24.1 27.4 %collective-permute-done = f32[290,30,50]{0,1,2:T(8,128)S(1)} collective-permute-done((f32[290,30,50]{0,1,2:T(8,128)}, f32[290,30,50]{0,1,2:T(8,128)S(1)}, u32[]{:S(2)}, u32[]{:S(2)}) %collective-permute-start) | collective-permute-done | bytes 1740032 | tf_op jit(solution)/shard_map/while/body/eval_jaxpr/ppermute | solution.py:34
  51.5 1.4 copy.42
  52.9 3.9 %fusion.25 = f32[30,8,30]{2,0,1:T(8,128)S(1)} fusion(f32[30,8,30]{2,0,1:T(8,128)S(1)} %get-tuple-element.206, s32[]{:T(128)S(6)} %select_n.61, f32[290,30,50]{0,1,2:T(8,128)} %get-tuple-element.216, f32[290,30,50]{0,1,2:T(8,128)S(1)} %collective-permute-done), kind=kOutput, calls=%fused_computation.1.clone.1 | convolution fusion | flops 156600000 | bytes 4213988 | tf_op jit(solution)/shard_map/while/body/eval_jaxpr/qmi,qni->mn/dot_general | solution.py:27
  56.8 3.1 %collective-permute-start = (f32[290,30,50]{0,1,2:T(8,128)}, f32[290,30,50]{0,1,2:T(8,128)S(1)}, u32[]{:S(2)}, u32[]{:S(2)}) collective-permute-start(f32[290,30,50]{0,1,2:T(8,128)} %get-tuple-element.205), channel_id=1, source_target_pairs={{0,7},{1,0},{2,1},{3,2},{4,3},{5,4},{6,5},{7,6},{8,15},{9,8},{10,9... | collective-permute-start | bytes 5220008 | tf_op jit(solution)/shard_map/while/body/eval_jaxpr/ppermute | solution.py:34
  59.9 27.4 %collective-permute-done = f32[290,30,50]{0,1,2:T(8,128)S(1)} collective-permute-done((f32[290,30,50]{0,1,2:T(8,128)}, f32[290,30,50]{0,1,2:T(8,128)S(1)}, u32[]{:S(2)}, u32[]{:S(2)}) %collective-permute-start) | collective-permute-done | bytes 1740032 | tf_op jit(solution)/shard_map/while/body/eval_jaxpr/ppermute | solution.py:34
  87.3 1.4 copy.42
  88.8 3.9 %fusion.25 = f32[30,8,30]{2,0,1:T(8,128)S(1)} fusion(f32[30,8,30]{2,0,1:T(8,128)S(1)} %get-tuple-element.206, s32[]{:T(128)S(6)} %select_n.61, f32[290,30,50]{0,1,2:T(8,128)} %get-tuple-element.216, f32[290,30,50]{0,1,2:T(8,128)S(1)} %collective-permute-done), kind=kOutput, calls=%fused_computation.1.clone.1 | convolution fusion | flops 156600000 | bytes 4213988 | tf_op jit(solution)/shard_map/while/body/eval_jaxpr/qmi,qni->mn/dot_general | solution.py:27
  92.6 3.1 %collective-permute-start = (f32[290,30,50]{0,1,2:T(8,128)}, f32[290,30,50]{0,1,2:T(8,128)S(1)}, u32[]{:S(2)}, u32[]{:S(2)}) collective-permute-start(f32[290,30,50]{0,1,2:T(8,128)} %get-tuple-element.205), channel_id=1, source_target_pairs={{0,7},{1,0},{2,1},{3,2},{4,3},{5,4},{6,5},{7,6},{8,15},{9,8},{10,9... | collective-permute-start | bytes 5220008 | tf_op jit(solution)/shard_map/while/body/eval_jaxpr/ppermute | solution.py:34
  95.8 27.4 %collective-permute-done = f32[290,30,50]{0,1,2:T(8,128)S(1)} collective-permute-done((f32[290,30,50]{0,1,2:T(8,128)}, f32[290,30,50]{0,1,2:T(8,128)S(1)}, u32[]{:S(2)}, u32[]{:S(2)}) %collective-permute-start) | collective-permute-done | bytes 1740032 | tf_op jit(solution)/shard_map/while/body/eval_jaxpr/ppermute | solution.py:34
  123.2 1.4 copy.42
  124.6 3.9 %fusion.25 = f32[30,8,30]{2,0,1:T(8,128)S(1)} fusion(f32[30,8,30]{2,0,1:T(8,128)S(1)} %get-tuple-element.206, s32[]{:T(128)S(6)} %select_n.61, f32[290,30,50]{0,1,2:T(8,128)} %get-tuple-element.216, f32[290,30,50]{0,1,2:T(8,128)S(1)} %collective-permute-done), kind=kOutput, calls=%fused_computation.1.clone.1 | convolution fusion | flops 156600000 | bytes 4213988 | tf_op jit(solution)/shard_map/while/body/eval_jaxpr/qmi,qni->mn/dot_general | solution.py:27
  128.4 3.1 %collective-permute-start = (f32[290,30,50]{0,1,2:T(8,128)}, f32[290,30,50]{0,1,2:T(8,128)S(1)}, u32[]{:S(2)}, u32[]{:S(2)}) collective-permute-start(f32[290,30,50]{0,1,2:T(8,128)} %get-tuple-element.205), channel_id=1, source_target_pairs={{0,7},{1,0},{2,1},{3,2},{4,3},{5,4},{6,5},{7,6},{8,15},{9,8},{10,9... | collective-permute-start | bytes 5220008 | tf_op jit(solution)/shard_map/while/body/eval_jaxpr/ppermute | solution.py:34
  131.6 27.4 %collective-permute-done = f32[290,30,50]{0,1,2:T(8,128)S(1)} collective-permute-done((f32[290,30,50]{0,1,2:T(8,128)}, f32[290,30,50]{0,1,2:T(8,128)S(1)}, u32[]{:S(2)}, u32[]{:S(2)}) %collective-permute-start) | collective-permute-done | bytes 1740032 | tf_op jit(solution)/shard_map/while/body/eval_jaxpr/ppermute | solution.py:34
  159.0 1.4 copy.42
  160.4 3.9 %fusion.25 = f32[30,8,30]{2,0,1:T(8,128)S(1)} fusion(f32[30,8,30]{2,0,1:T(8,128)S(1)} %get-tuple-element.206, s32[]{:T(128)S(6)} %select_n.61, f32[290,30,50]{0,1,2:T(8,128)} %get-tuple-element.216, f32[290,30,50]{0,1,2:T(8,128)S(1)} %collective-permute-done), kind=kOutput, calls=%fused_computation.1.clone.1 | convolution fusion | flops 156600000 | bytes 4213988 | tf_op jit(solution)/shard_map/while/body/eval_jaxpr/qmi,qni->mn/dot_general | solution.py:27
  164.3 0.1 copy.21
  164.4 0.8 reshape.42
  165.2 4.4 %all-to-all-start = ((f32[8,1,900]{2,1,0:T(1,128)}), f32[8,1,900]{2,1,0:T(1,128)S(1)}, u32[]{:S(2)}, u32[]{:S(2)}) async-start(f32[8,1,900]{2,1,0:T(1,128)} %reshape.42), calls=%async_computation | async-start | bytes 65536 | tf_op jit(solution)/shard_map/all_to_all | solution.py:41
  169.6 10.1 %copy.16 = f32[290,30,240]{2,1,0:T(8,128)} copy(f32[290,30,240]{2,0,1:T(8,128)} %param.4) | data formatting | bytes 16704000 | tf_op args[0]
  179.7 0.3 convolution_bitcast_fusion.1
  180.0 9.9 %convolution_reduce_fusion = f32[290]{0:T(512)S(1)} fusion(f32[290,30,240]{2,0,1:T(8,128)} %param.4, f32[30,240,1]{1,0,2:T(8,128)S(1)} %convolution_bitcast_fusion.1), kind=kOutput, calls=%fused_computation.7 | convolution fusion | flops 25056000 | bytes 8381960 | tf_op jit(solution)/shard_map/dot_general | solution.py:21
  190.0 15.6 %psum.7 = f32[290]{0:T(512)S(1)} all-reduce(f32[290]{0:T(512)S(1)} %convolution_reduce_fusion), channel_id=1, replica_groups=mesh['sys'=1,'aux'=4,'orb'=8] {'orb'}, use_global_device_ids=true, to_apply=%region_0.0 | all-reduce | flops 290 | bytes 2320 | tf_op jit(solution)/shard_map/psum | solution.py:22
  205.6 10.8 %reshape.29 = f32[290,7200]{1,0:T(8,128)} reshape(f32[290,30,240]{2,1,0:T(8,128)} %copy.16) | data formatting | bytes 16704000 | tf_op jit(solution)/shard_map/reshape | solution.py:20
  216.4 12.9 %dot_general.32 = f32[30,240,290]{1,0,2:T(8,128)} reshape(f32[7200,290]{0,1:T(8,128)} %bitcast.42) | data formatting | bytes 16704000 | tf_op jit(solution)/shard_map/dot_general | solution.py:23
  229.3 0.0 copy-start.1
  229.3 13.3 %fusion.1 = f32[1,30,240]{2,0,1:T(1,128)S(1)} fusion(f32[290,1,1]{0,1,2:T(1,128)S(1)} %reshape.34, f32[30,240,290]{1,0,2:T(8,128)} %dot_general.32), kind=kOutput, calls=%fused_computation.2 | convolution fusion | flops 25056000 | bytes 8381960 | tf_op jit(solution)/shard_map/dot_general | solution.py:23
  242.6 0.0 copy-done.1
  242.6 0.6 dynamic-slice
  243.8 0.0 all-to-all-done
  243.8 0.5 broadcast.42
  244.4 0.7 reduce.2
  245.1 0.1 reshape.43
  245.2 0.1 bitcast_select_fusion
  245.3 0.1 copy.22
  245.4 0.1 reshape.30
  245.5 19.0 %all-reduce = f32[30,240]{1,0:T(8,128)S(1)} all-reduce(f32[30,240]{1,0:T(8,128)S(1)} %fusion.6), channel_id=2, replica_groups=mesh['sys'=1,'aux'=4,'orb'=8] {'aux'}, use_global_device_ids=true, to_apply=%region_3.4.clone | all-reduce | flops 7200 | bytes 57600
  264.5 0.7 constant_dynamic-slice_fusion
  (4 shorter events, 0.0 us)
Async XLA Ops:
  0.0 0.8 copy-start
  22.0 29.5 %collective-permute-start = (f32[290,30,50]{0,1,2:T(8,128)}, f32[290,30,50]{0,1,2:T(8,128)S(1)}, u32[]{:S(2)}, u32[]{:S(2)}) collective-permute-start(f32[290,30,50]{0,1,2:T(8,128)} %get-tuple-element.205), channel_id=1, source_target_pairs={{0,7},{1,0},{2,1},{3,2},{4,3},{5,4},{6,5},{7,6},{8,15},{9,8},{10,9... | collective-permute-start | bytes 5220008 | tf_op jit(solution)/shard_map/while/body/eval_jaxpr/ppermute | solution.py:34
  56.8 30.5 %collective-permute-start = (f32[290,30,50]{0,1,2:T(8,128)}, f32[290,30,50]{0,1,2:T(8,128)S(1)}, u32[]{:S(2)}, u32[]{:S(2)}) collective-permute-start(f32[290,30,50]{0,1,2:T(8,128)} %get-tuple-element.205), channel_id=1, source_target_pairs={{0,7},{1,0},{2,1},{3,2},{4,3},{5,4},{6,5},{7,6},{8,15},{9,8},{10,9... | collective-permute-start | bytes 5220008 | tf_op jit(solution)/shard_map/while/body/eval_jaxpr/ppermute | solution.py:34
  92.6 30.5 %collective-permute-start = (f32[290,30,50]{0,1,2:T(8,128)}, f32[290,30,50]{0,1,2:T(8,128)S(1)}, u32[]{:S(2)}, u32[]{:S(2)}) collective-permute-start(f32[290,30,50]{0,1,2:T(8,128)} %get-tuple-element.205), channel_id=1, source_target_pairs={{0,7},{1,0},{2,1},{3,2},{4,3},{5,4},{6,5},{7,6},{8,15},{9,8},{10,9... | collective-permute-start | bytes 5220008 | tf_op jit(solution)/shard_map/while/body/eval_jaxpr/ppermute | solution.py:34
  128.4 30.5 %collective-permute-start = (f32[290,30,50]{0,1,2:T(8,128)}, f32[290,30,50]{0,1,2:T(8,128)S(1)}, u32[]{:S(2)}, u32[]{:S(2)}) collective-permute-start(f32[290,30,50]{0,1,2:T(8,128)} %get-tuple-element.205), channel_id=1, source_target_pairs={{0,7},{1,0},{2,1},{3,2},{4,3},{5,4},{6,5},{7,6},{8,15},{9,8},{10,9... | collective-permute-start | bytes 5220008 | tf_op jit(solution)/shard_map/while/body/eval_jaxpr/ppermute | solution.py:34
  165.2 78.6 %all-to-all-start = ((f32[8,1,900]{2,1,0:T(1,128)}), f32[8,1,900]{2,1,0:T(1,128)S(1)}, u32[]{:S(2)}, u32[]{:S(2)}) async-start(f32[8,1,900]{2,1,0:T(1,128)} %reshape.42), calls=%async_computation | async-start | bytes 65536 | tf_op jit(solution)/shard_map/all_to_all | solution.py:41
  229.3 13.3 %copy-start.1 = (u32[32]{0:T(128)S(1)}, u32[32]{0:T(128)}, u32[]{:S(2)}) copy-start(u32[32]{0:T(128)} %constant.81) | copy-start | bytes 388
where the time goes:
time: 266 us; the launch traced here: 265 us
  waiting for transfers between devices  110 us (41%)
  matrix products  54.9 us (21%)
  local copies, waits for them, and re-layouts  48.6 us (18%)
  blocking collectives  34.6 us (13%)
  starting transfers between devices  16 us (6%)
    ppermute x4, waiting for transfers between devices, pass_step(): t_moving = lax.ppermute(t_moving, 'orb', shift_perm)  110 us
    dot_general x5, matrix products, exch_block(): jnp.einsum('qmi,qni->mn', half_t, t_other, precision=PREC_MODE, preferred...  20 us
    unnamed x1, blocking collectives  19 us
    unnamed x10, local copies, waits for them, and re-layouts  16.4 us
    psum x1, blocking collectives, local_fock(): aux_coef = lax.psum(coef_part, 'orb')  15.6 us
    dot_general x1, matrix products, local_fock(): jnp.dot(aux_coef, fit_flat, precision=PREC_MODE, preferred_element_type=j...  13.3 us
    dot_general x1, local copies, waits for them, and re-layouts, local_fock(): jnp.dot(aux_coef, fit_flat, precision=PREC_MODE, preferred_element_type=j...  12.9 us
    ppermute x4, starting transfers between devices, pass_step(): t_moving = lax.ppermute(t_moving, 'orb', shift_perm)  11.6 us
  transfers between devices with their start and end apart: 5, of which 4 were waited for; matrix products, arithmetic and copies ran while one was open for 22% of the time, Pallas kernels for 0%

commit v1 on v0

v1 whole, which is shorter than its diff:
```python
import functools
import jax
import jax.numpy as jnp
from jax import lax
from jax.experimental import pallas as pl
from jax.experimental.pallas import tpu as pltpu
from jax.sharding import PartitionSpec as P

PREC_MODE = lax.Precision.HIGHEST
MESH_ID = pl.DeviceIdType.MESH
LANES = 128
SUBL = 8


def mm(lhs, rhs, lhs_dim, rhs_dim):
    return lax.dot_general(lhs, rhs, (((lhs_dim,), (rhs_dim,)), ((), ())), precision=PREC_MODE, preferred_element_type=jnp.float32)


def rup(value, unit):
    return -(-value // unit) * unit


def fock_kernel(dims, fit_ref, occ_ref, out_ref, bv, ct, dens, recv, send, ex_send, ex_recv, xs, kacc,
                srow, gsend, grecv, gbc, jsend, jrecv, ksend, krecv,
                load_sem, t_ss, t_rs, l_ss, l_rs, g_ss, g_rs, j_ss, j_rs, k_ss, k_rs):
    n_orb, n_aux, q_loc, row_blk, n_bf, n_occ, row_pad, occ_pad, occ_main, q_tile, rounds, q_left, left_base, left_row, n_cols = dims
    me = lax.axis_index('orb')
    my = lax.axis_index('aux')
    n_dev = n_orb * n_aux

    def peer_orb(step):
        return lax.rem(me + step, n_orb)

    def loads():
        for rd, (q_base, tiles, t_base) in enumerate(rounds):
            size = tiles * q_tile * n_orb + (q_left if rd == len(rounds) - 1 else 0)
            yield pltpu.make_async_copy(fit_ref.at[pl.ds(q_base, size)], bv.at[pl.ds(q_base, size)], load_sem.at[rd])

    load_list = list(loads())
    for cp in load_list:
        cp.start()

    ex_send[...] = jnp.zeros(ex_send.shape, jnp.float32)
    ex_recv[me] = jnp.zeros(ex_recv.shape[1:], jnp.float32)
    barrier = pltpu.get_barrier_semaphore()

    def greet(step, carry):
        pl.semaphore_signal(barrier, inc=1, device_id={'orb': lax.rem(me + lax.rem(step, n_orb), n_orb), 'aux': lax.rem(my + step // n_orb, n_aux)}, device_id_type=MESH_ID)
        return carry

    lax.fori_loop(1, n_dev, greet, 0)

    occ = occ_ref[...]

    def rows_of_ct(count, scale, shift):
        row = lax.broadcasted_iota(jnp.int32, (count, n_occ), 0)
        col = lax.broadcasted_iota(jnp.int32, (count, n_occ), 1)
        return mm((row * scale + shift == col).astype(jnp.float32), occ, 1, 1)

    half_occ = rup(n_occ, 2 * SUBL) // 2
    ct[0:occ_pad, :] = rows_of_ct(occ_pad, 1, 0)
    ct[occ_pad:occ_pad + half_occ, :] = rows_of_ct(half_occ, 2, 0)
    ct[occ_pad + half_occ:, :] = rows_of_ct(half_occ, 2, 1)
    pick = lax.broadcasted_iota(jnp.int32, (row_blk, n_bf), 0)
    pick_col = lax.broadcasted_iota(jnp.int32, (row_blk, n_bf), 1)
    own = mm((pick + me * row_blk == pick_col).astype(jnp.float32), occ, 1, 0)
    dens[...] = mm(own, occ, 1, 1)

    n_rounds = len(rounds)

    def t_copy(rd, dst, src_dev):
        q_base, tiles, t_base = rounds[rd]
        return pltpu.make_async_remote_copy(
            src_ref=send.at[dst, pl.ds(t_base, tiles)],
            dst_ref=recv.at[src_dev, pl.ds(t_base, tiles)],
            send_sem=t_ss.at[rd, dst], recv_sem=t_rs.at[rd, src_dev],
            device_id={'orb': dst}, device_id_type=MESH_ID)

    def padded_rows(q_start, n_q):
        block = bv[pl.ds(q_start, n_q)]
        block = jnp.concatenate([block, jnp.zeros((n_q, row_pad - row_blk, n_bf), jnp.float32)], axis=1)
        return block.reshape(n_q * row_pad, n_bf)

    def t_block(rd, dst, into, into_ex):
        q_base, tiles, t_base = rounds[rd]
        n_q = tiles * q_tile
        block = mm(ct[0:occ_pad, :], padded_rows(q_base + dst * n_q, n_q), 1, 1)
        extra = n_occ - occ_main
        for tile in range(tiles):
            piece = block[:, tile * LANES:(tile + 1) * LANES]
            into[dst, t_base + tile] = piece[0:occ_main]
            at = (t_base + tile) * extra
            into_ex[dst, at:at + extra, :] = piece[occ_main:n_occ]

    def t_round(rd, first):
        q_base, tiles, t_base = rounds[rd]
        load_list[rd].wait()

        def step(r, carry):
            dst = peer_orb(r)
            t_block(rd, dst, send, ex_send)

            @pl.when(r > 1)
            def _():
                t_copy(rd, peer_orb(r - 1), me).start()
            return carry

        if first:
            step(1, 0)
            pl.semaphore_wait(barrier, n_dev - 1)
            lax.fori_loop(2, n_orb, step, 0)
        else:
            lax.fori_loop(1, n_orb, step, 0)
        t_block(rd, me, recv, ex_recv)
        t_copy(rd, peer_orb(n_orb - 1), me).start()

    def l_copy(dst, src_dev):
        return pltpu.make_async_remote_copy(
            src_ref=ex_send.at[dst], dst_ref=ex_recv.at[src_dev], send_sem=l_ss.at[dst], recv_sem=l_rs.at[src_dev],
            device_id={'orb': dst}, device_id_type=MESH_ID)

    def g_copy(dst, src_dev):
        return pltpu.make_async_remote_copy(
            src_ref=gsend, dst_ref=grecv.at[src_dev], send_sem=g_ss.at[dst], recv_sem=g_rs.at[src_dev],
            device_id={'orb': dst}, device_id_type=MESH_ID)

    def j_copy(dst, src_dev):
        return pltpu.make_async_remote_copy(
            src_ref=jsend.at[dst], dst_ref=jrecv.at[src_dev], send_sem=j_ss.at[dst], recv_sem=j_rs.at[src_dev],
            device_id={'aux': dst}, device_id_type=MESH_ID)

    def k_copy(orb, aux, src_dev):
        slot = aux * n_orb + orb
        return pltpu.make_async_remote_copy(
            src_ref=ksend.at[slot], dst_ref=krecv.at[src_dev], send_sem=k_ss.at[slot], recv_sem=k_rs.at[src_dev],
            device_id={'orb': orb, 'aux': aux}, device_id_type=MESH_ID)

    def gamma_part():
        for cp in load_list[2:]:
            cp.wait()

        def body(q, carry):
            srow[pl.ds(q, 1), :] = jnp.sum(bv[q] * dens[...], axis=0, keepdims=True)
            return carry

        lax.fori_loop(0, q_loc, body, 0, unroll=10)
        total = jnp.zeros((SUBL, LANES), jnp.float32)
        for k in range(srow.shape[0] // LANES):
            row_k = (lax.broadcasted_iota(jnp.int32, (SUBL, n_bf), 0) == k).astype(jnp.float32)
            total = total + mm(row_k, srow[k * LANES:(k + 1) * LANES, :], 1, 1)
        gsend[...] = total
        grecv[me] = total

    def gamma_send():
        for r in range(1, n_orb):
            g_copy(peer_orb(r), me).start()

    def coulomb():
        for r in range(1, n_orb):
            g_copy(me, peer_orb(r)).wait_recv()
        gam = grecv[0]
        for src in range(1, n_orb):
            gam = gam + grecv[src]
        for k in range(srow.shape[0] // LANES):
            row_k = (lax.broadcasted_iota(jnp.int32, (SUBL, n_bf), 0) == k).astype(jnp.float32)
            gbc[k * LANES:(k + 1) * LANES, :] = mm(gam, row_k, 0, 0)

        def body(q, acc):
            return acc + bv[q] * gbc[pl.ds(q, 1), :]

        jfull = lax.fori_loop(0, q_loc, body, jnp.zeros((row_blk, n_bf), jnp.float32), unroll=10)
        jpad = jnp.concatenate([jfull, jnp.zeros((row_blk, 2 * LANES - n_bf), jnp.float32)], axis=1)
        for a in range(n_aux):
            piece = jpad if a == 0 else pltpu.roll(jpad, 2 * LANES - a * n_cols, 1)
            jsend[a, 0:row_blk, :] = piece[:, 0:LANES]
        jrecv[my] = jsend[my]
        for r in range(1, n_aux):
            j_copy(lax.rem(my + r, n_aux), my).start()

    lane = lax.broadcasted_iota(jnp.int32, (occ_main, LANES), 1)

    def regroup(parts):
        rows = parts[0].shape[0]
        ln = lane[0:rows]
        low = ln < 2 * row_pad
        even = (ln // row_pad) % 2 == 0
        a0, a1, a2, a3 = parts
        b0 = jnp.where(low, a0, pltpu.roll(a2, 2 * row_pad, 1))
        b2 = jnp.where(low, pltpu.roll(a0, 2 * row_pad, 1), a2)
        b1 = jnp.where(low, a1, pltpu.roll(a3, 2 * row_pad, 1))
        b3 = jnp.where(low, pltpu.roll(a1, 2 * row_pad, 1), a3)
        back = LANES - row_pad
        return [jnp.where(even, b0, pltpu.roll(b1, row_pad, 1)), jnp.where(even, pltpu.roll(b0, back, 1), b1),
                jnp.where(even, b2, pltpu.roll(b3, row_pad, 1)), jnp.where(even, pltpu.roll(b2, back, 1), b3)]

    def exchange_round(rd):
        q_base, tiles, t_base = rounds[rd]
        last = rd == n_rounds - 1
        for r in range(1, n_orb):
            t_copy(rd, me, peer_orb(r)).wait_recv()
        if last:
            for r in range(1, n_orb):
                l_copy(me, peer_orb(r)).wait_recv()
        depth = tiles * q_tile * occ_main
        n_ex = ex_recv.shape[1]
        for grp in range(n_orb // q_tile):
            cols = slice(grp * LANES, (grp + 1) * LANES)
            for tile in range(tiles):
                outs = regroup([recv[grp * q_tile + j, t_base + tile] for j in range(q_tile)])
                for q in range(q_tile):
                    base = (tile * q_tile + q) * occ_main
                    xs[base:base + occ_main, cols] = outs[q]
            if last:
                outs = regroup([ex_recv[grp * q_tile + j] for j in range(q_tile)])
                for q in range(q_tile):
                    xs[depth + q * n_ex:depth + (q + 1) * n_ex, cols] = outs[q]
        if last:
            depth += q_tile * n_ex
        xv = xs[0:depth, :]
        part = mm(xv, xv, 0, 0)
        kacc[...] = part if rd == 0 else kacc[...] + part

    t_round(0, True)
    t_round(1, False)
    gamma_part()
    class Done:
        def wait(self):
            pass
    for rd in range(2, n_rounds):
        load_list[rd] = Done()
    t_round(2, False)
    gamma_send()
    t_round(3, False)
    coulomb()
    t_round(4, False)
    left_rows = padded_rows(left_base, q_left)
    left_rows = jnp.concatenate([left_rows, left_rows], axis=0)
    first = lax.broadcasted_iota(jnp.int32, (half_occ, LANES), 1) < LANES // 2
    left = jnp.where(first, mm(ct[occ_pad:occ_pad + half_occ, :], left_rows, 1, 1), mm(ct[occ_pad + half_occ:, :], left_rows, 1, 1))
    share = half_occ // n_orb
    for dst in range(n_orb):
        ex_send[dst, left_row:left_row + share, :] = left[dst * share:(dst + 1) * share, :]
    ex_recv[me, left_row:left_row + share, :] = ex_send[me, left_row:left_row + share, :]
    exchange_round(0)
    for r in range(1, n_orb):
        l_copy(peer_orb(r), me).start()
    for rd in range(1, n_rounds):
        exchange_round(rd)

    half = row_pad // 2
    low_half = lax.broadcasted_iota(jnp.int32, (half, LANES), 1) < LANES // 2
    for orb in range(n_orb):
        for ctile in range(n_aux // 2):
            blk = kacc[orb * row_pad:(orb + 1) * row_pad, ctile * LANES:(ctile + 1) * LANES]
            top, bot = blk[0:half], blk[half:]
            ksend[2 * ctile * n_orb + orb] = jnp.where(low_half, top, pltpu.roll(bot, LANES // 2, 1))
            ksend[(2 * ctile + 1) * n_orb + orb] = jnp.where(low_half, pltpu.roll(top, LANES // 2, 1), bot)
    dev = my * n_orb + me
    krecv[dev] = ksend[dev]

    def k_send(step, carry):
        k_copy(lax.rem(me + lax.rem(step, n_orb), n_orb), lax.rem(my + step // n_orb, n_aux), dev).start()
        return carry

    lax.fori_loop(1, n_dev, k_send, 0)
    for r in range(1, n_aux):
        j_copy(my, lax.rem(my + r, n_aux)).wait_recv()
    jsum = jrecv[0]
    for src in range(1, n_aux):
        jsum = jsum + jrecv[src]

    def k_wait(step, carry):
        src = lax.rem(my + step // n_orb, n_aux) * n_orb + lax.rem(me + lax.rem(step, n_orb), n_orb)
        k_copy(me, my, src).wait_recv()
        return carry

    lax.fori_loop(1, n_dev, k_wait, 0)
    ksum = krecv[0]
    for src in range(1, n_dev):
        ksum = ksum + krecv[src]
    kblk = jnp.concatenate([ksum, pltpu.roll(ksum, LANES // 2, 1)], axis=0)
    pad_cols = row_pad - row_blk
    kcols = jnp.where(lax.broadcasted_iota(jnp.int32, (row_pad, LANES), 1) < row_blk, kblk, pltpu.roll(kblk, LANES - pad_cols, 1))
    out = 2.0 * jsum - kcols
    out_ref[...] = out[0:row_blk, 0:n_cols]

    for rd in range(n_rounds):
        for r in range(1, n_orb):
            t_copy(rd, peer_orb(r), me).wait_send()
    for r in range(1, n_orb):
        l_copy(peer_orb(r), me).wait_send()
        g_copy(peer_orb(r), me).wait_send()
    for r in range(1, n_aux):
        j_copy(lax.rem(my + r, n_aux), my).wait_send()

    def k_drain(step, carry):
        k_copy(lax.rem(me + lax.rem(step, n_orb), n_orb), lax.rem(my + step // n_orb, n_aux), dev).wait_send()
        return carry

    lax.fori_loop(1, n_dev, k_drain, 0)


def solution(mesh):
    n_orb = mesh.shape['orb']
    n_aux = mesh.shape['aux']

    def local_fock(fit_loc, orbitals):
        q_loc, row_blk, n_bf = fit_loc.shape
        n_occ = orbitals.shape[1]
        n_cols = n_bf // n_aux
        row_pad = 32
        q_tile = LANES // row_pad
        occ_pad = rup(n_occ, SUBL)
        occ_main = n_occ // SUBL * SUBL
        all_tiles = q_loc // (q_tile * n_orb)
        rounds, q_base, t_base = [], 0, 0
        while t_base < all_tiles:
            tiles = min(2, all_tiles - t_base)
            rounds.append((q_base, tiles, t_base))
            q_base += tiles * q_tile * n_orb
            t_base += tiles
        q_left = q_loc - q_base
        left_row = all_tiles * (n_occ - occ_main)
        half_occ = rup(n_occ, 2 * SUBL) // 2
        ex_rows = rup(left_row + half_occ // n_orb, SUBL)
        assert row_blk <= row_pad and n_orb % q_tile == 0 and n_orb == 2 * n_aux and n_cols == 2 * row_blk
        assert 2 * q_left == q_tile and occ_main < n_occ and half_occ % n_orb == 0
        dims = (n_orb, n_aux, q_loc, row_blk, n_bf, n_occ, row_pad, occ_pad, occ_main, q_tile, tuple(rounds), q_left, q_base, left_row, n_cols)
        n_dev = n_orb * n_aux
        n_rounds = len(rounds)
        q_lanes = rup(q_loc, LANES)
        depth_max = max(2 * q_tile * occ_main, q_tile * (occ_main + ex_rows))
        f32 = jnp.float32
        dma = pltpu.SemaphoreType.DMA
        scratch = [
            pltpu.VMEM((q_loc, row_blk, n_bf), f32),
            pltpu.VMEM((occ_pad + 2 * half_occ, n_bf), f32),
            pltpu.VMEM((row_blk, n_bf), f32),
            pltpu.VMEM((n_orb, all_tiles, occ_main, LANES), f32),
            pltpu.VMEM((n_orb, all_tiles, occ_main, LANES), f32),
            pltpu.VMEM((n_orb, ex_rows, LANES), f32),
            pltpu.VMEM((n_orb, ex_rows, LANES), f32),
            pltpu.VMEM((depth_max, n_orb * row_pad), f32),
            pltpu.VMEM((n_orb * row_pad, n_orb * row_pad), f32),
            pltpu.VMEM((q_lanes, n_bf), f32),
            pltpu.VMEM((SUBL, LANES), f32),
            pltpu.VMEM((n_orb, SUBL, LANES), f32),
            pltpu.VMEM((q_lanes, n_bf), f32),
            pltpu.VMEM((n_aux, row_pad, LANES), f32),
            pltpu.VMEM((n_aux, row_pad, LANES), f32),
            pltpu.VMEM((n_dev, row_pad // 2, LANES), f32),
            pltpu.VMEM((n_dev, row_pad // 2, LANES), f32),
            dma((n_rounds,)), dma((n_rounds, n_orb)), dma((n_rounds, n_orb)), dma((n_orb,)), dma((n_orb,)),
            dma((n_orb,)), dma((n_orb,)), dma((n_aux,)), dma((n_aux,)), dma((n_dev,)), dma((n_dev,)),
        ]
        return pl.pallas_call(
            functools.partial(fock_kernel, dims),
            out_shape=jax.ShapeDtypeStruct((row_blk, n_cols), f32),
            in_specs=[pl.BlockSpec(memory_space=pl.ANY), pl.BlockSpec(memory_space=pltpu.VMEM)],
            out_specs=pl.BlockSpec(memory_space=pltpu.VMEM),
            scratch_shapes=scratch,
            compiler_params=pltpu.CompilerParams(collective_id=0, has_side_effects=True, vmem_limit_bytes=48 * 1024 * 1024),
            name='fock_build',
        )(fit_loc, orbitals)

    spec_fit = P(('sys', 'aux'), 'orb', None)
    spec_orbitals = P('sys', None)
    spec_out = P(('sys', 'orb'), 'aux')
    return jax.shard_map(local_fock, mesh=mesh, in_specs=(spec_fit, spec_orbitals), out_specs=spec_out, check_vma=False)
```

time: 266 us -> 57.9 us (0.22)
  the two profiles are of different devices: /device:TPU:96 before, /device:TPU:97 now
where the time goes in v1:
time: 57.9 us; the launch traced here: 57.7 us
  Pallas kernels  46.1 us (80%)
  local copies, waits for them, and re-layouts  11.6 us (20%)
    pallas_call x1, Pallas kernels, local_fock(): pl.pallas_call(functools.partial(fock_kernel, dims), out_shape=jax.ShapeD...  46.1 us
    unnamed x3, local copies, waits for them, and re-layouts  11.6 us

profile of v1, /device:TPU:97, one launch (start us, length us, event | category | flops | bytes accessed | tf_op | source)
XLA Modules:
  0.0 57.7 jit_solution(10396573692274251686)
XLA Ops:
  0.0 0.9 %copy.4.occ_ref = f32[240,50]{1,0:T(8,128)S(1)} copy(f32[240,50]{0,1:T(8,128)} %param.3) | data formatting | bytes 96000 | tf_op args[1]
  0.9 10.1 %copy.3.fit_ref = f32[290,30,240]{2,1,0:T(8,128)} copy(f32[290,30,240]{2,0,1:T(8,128)} %param.2) | data formatting | bytes 16704000 | tf_op args[0]
  11.0 46.1 %fock_build.1 = f32[30,60]{1,0:T(8,128)S(1)} custom-call(f32[290,30,240]{2,1,0:T(8,128)} %copy.3.fit_ref, f32[240,50]{1,0:T(8,128)S(1)} %copy.4.occ_ref), custom_call_target="tpu_custom_call" | custom-call | tf_op jit(solution)/shard_map/fock_build/pallas_call | solution.py:356
  57.1 0.6 %copy.6 = f32[30,60]{1,0:T(8,128)} copy(f32[30,60]{1,0:T(8,128)S(1)} %fock_build.1) | data formatting | bytes 14400

commit v2 on v0

v2 whole, which is shorter than its diff:
```python
import functools
import jax
import jax.numpy as jnp
from jax import lax
from jax.experimental import pallas as pl
from jax.experimental.pallas import tpu as pltpu
from jax.sharding import PartitionSpec as P

PREC_MODE = lax.Precision.HIGHEST
MESH_ID = pl.DeviceIdType.MESH
LANES = 128
SUBL = 8


ORDER = (4, 2, 6, 5, 3, 7, 1)


def mm(lhs, rhs, lhs_dim, rhs_dim):
    return lax.dot_general(lhs, rhs, (((lhs_dim,), (rhs_dim,)), ((), ())), precision=PREC_MODE, preferred_element_type=jnp.float32)


def rup(value, unit):
    return -(-value // unit) * unit


class Loaded:
    def wait(self):
        pass


def fock_kernel(dims, fit_ref, occ_ref, out_ref, bv, ct, ctp, ctl, dens, recv, send, ex_recv, ex_send, xa, kacc,
                srow, gsend, grecv, gbc, jrows, jsend, jrecv, ksend, krecv,
                load_sem, t_ss, t_rs, l_ss, l_rs, g_ss, g_rs, j_ss, j_rs, k_ss, k_rs):
    (n_orb, n_aux, q_loc, row_blk, n_bf, n_occ, row_pad, occ_each, groups, q_main, left_pad, fold, n_cols) = dims
    me = lax.axis_index('orb')
    my = lax.axis_index('aux')
    n_dev = n_orb * n_aux
    n_tiles = q_main // LANES
    slots = n_tiles * occ_each
    n_groups = len(groups)
    q_left = q_loc - q_main
    whole = row_blk // SUBL * SUBL
    rest = row_blk - whole
    pairs = occ_each // fold
    extra = n_occ - n_orb * occ_each

    def peer_orb(step):
        return lax.rem(me + step, n_orb)

    occ_load = pltpu.make_async_copy(occ_ref, ct, load_sem.at[n_groups])
    occ_load.start()
    load_list = [pltpu.make_async_copy(fit_ref.at[pl.ds(m0, mg)], bv.at[pl.ds(m0, mg)], load_sem.at[g]) for g, (m0, mg, base) in enumerate(groups)]
    for cp in load_list:
        cp.start()

    barrier = pltpu.get_barrier_semaphore()

    def greet(step, carry):
        pl.semaphore_signal(barrier, inc=1, device_id={'orb': lax.rem(me + lax.rem(step, n_orb), n_orb), 'aux': lax.rem(my + step // n_orb, n_aux)}, device_id_type=MESH_ID)
        return carry

    lax.fori_loop(1, n_dev, greet, 0)
    ex_send[...] = jnp.zeros(ex_send.shape, jnp.float32)

    occ_load.wait()
    occ_t = ct[...]

    def rows_of_ct(which):
        return mm(which.astype(jnp.float32), occ_t, 1, 0)

    row = lax.broadcasted_iota(jnp.int32, (n_orb * SUBL, n_occ), 0)
    col = lax.broadcasted_iota(jnp.int32, (n_orb * SUBL, n_occ), 1)
    in_blk = row % SUBL
    ctp[...] = rows_of_ct(((in_blk < occ_each) & (col == row // SUBL * occ_each + in_blk))
                          | ((in_blk == occ_each) & (col == n_orb * occ_each + row // SUBL % extra)))
    rows_l = ctl.shape[0] // fold
    row = lax.broadcasted_iota(jnp.int32, (rows_l, n_occ), 0)
    col = lax.broadcasted_iota(jnp.int32, (rows_l, n_occ), 1)
    for j in range(fold):
        ctl[j * rows_l:(j + 1) * rows_l, :] = rows_of_ct((row <= pairs * n_orb) & (col == row * fold + j))
    pick = lax.broadcasted_iota(jnp.int32, (row_blk, n_bf), 0)
    pick_col = lax.broadcasted_iota(jnp.int32, (row_blk, n_bf), 1)
    own = mm((pick + me * row_blk == pick_col).astype(jnp.float32), occ_t, 1, 1)
    dens[...] = mm(own, occ_t, 1, 0)

    def t_copy(g, dst, src_dev):
        m0, mg, base = groups[g]
        return pltpu.make_async_remote_copy(
            src_ref=send.at[dst, pl.ds(base, slots * mg)], dst_ref=recv.at[src_dev, pl.ds(base, slots * mg)],
            send_sem=t_ss.at[g, dst], recv_sem=t_rs.at[g, src_dev], device_id={'orb': dst}, device_id_type=MESH_ID)

    def l_copy(dst, src_dev):
        return pltpu.make_async_remote_copy(
            src_ref=ex_send.at[dst], dst_ref=ex_recv.at[src_dev], send_sem=l_ss.at[dst], recv_sem=l_rs.at[src_dev],
            device_id={'orb': dst}, device_id_type=MESH_ID)

    def g_copy(dst, src_dev):
        return pltpu.make_async_remote_copy(
            src_ref=gsend, dst_ref=grecv.at[src_dev], send_sem=g_ss.at[dst], recv_sem=g_rs.at[src_dev],
            device_id={'orb': dst}, device_id_type=MESH_ID)

    def j_copy(dst, src_dev):
        return pltpu.make_async_remote_copy(
            src_ref=jsend.at[dst], dst_ref=jrecv.at[src_dev], send_sem=j_ss.at[dst], recv_sem=j_rs.at[src_dev],
            device_id={'aux': dst}, device_id_type=MESH_ID)

    def k_copy(orb, aux, src_dev):
        slot = aux * n_orb + orb
        return pltpu.make_async_remote_copy(
            src_ref=ksend.at[slot], dst_ref=krecv.at[src_dev], send_sem=k_ss.at[slot], recv_sem=k_rs.at[src_dev],
            device_id={'orb': orb, 'aux': aux}, device_id_type=MESH_ID)

    def ex_row(slot, m, tail):
        return (n_ex * whole + slot * rest + m - whole) if tail else (slot * whole + m)

    n_ex = pairs + 1

    def t_rows(g):
        m0, mg, base = groups[g]
        tail = m0 >= whole
        load_list[g].wait()

        def step(m, carry):
            block = mm(ctp[...], bv[m, 0:q_main, :], 1, 1)
            for d in range(n_orb):
                for t in range(n_tiles):
                    piece = block[d * SUBL:d * SUBL + occ_each, t * LANES:(t + 1) * LANES]
                    send[d, pl.ds(base + t * occ_each * mg + m - m0, occ_each, stride=mg), :] = piece
                    if d // extra == t:
                        at = d * SUBL + occ_each
                        ex_send[d, pl.ds(ex_row(pairs, m, tail), 1), :] = block[at:at + 1, t * LANES:(t + 1) * LANES]
            return carry

        lax.fori_loop(m0, m0 + mg, step, 0)

    def t_send(g):
        for r in ORDER:
            t_copy(g, peer_orb(r), me).start()
        m0, mg, base = groups[g]
        recv[me, base:base + slots * mg, :] = send[me, base:base + slots * mg, :]

    def left_rows():
        for m0, m1 in ((0, whole), (whole, row_blk)):
            tail = m0 >= whole

            def step(m, carry):
                rows = jnp.concatenate([bv[m, q_main:q_loc, :], jnp.zeros((left_pad - q_left, n_bf), jnp.float32)], axis=0)
                block = mm(ctl[...], rows, 1, 1)
                block = jnp.concatenate([block, jnp.zeros((fold * rows_l, LANES - left_pad), jnp.float32)], axis=1)
                total = block[0:rows_l]
                for j in range(1, fold):
                    total = total + pltpu.roll(block[j * rows_l:(j + 1) * rows_l], j * left_pad, 1)
                for d in range(n_orb):
                    for u in range(pairs):
                        ex_send[d, pl.ds(ex_row(u, m, tail), 1), :] = total[d * pairs + u:d * pairs + u + 1]
                d = n_tiles * extra
                ex_send[d, pl.ds(ex_row(pairs, m, tail), 1), :] = total[n_orb * pairs:n_orb * pairs + 1]
                return carry

            lax.fori_loop(m0, m1, step, 0)

    def gamma_part():
        q_step = 5 * SUBL
        for q0 in range(0, q_loc, q_step):
            n_q = min(q_step, q_loc - q0)

            def body(m, acc):
                return acc + bv[m, q0:q0 + n_q, :] * dens[pl.ds(m, 1), :]

            srow[q0:q0 + n_q, :] = lax.fori_loop(0, row_blk, body, jnp.zeros((n_q, n_bf), jnp.float32), unroll=3)
        total = jnp.zeros(gsend.shape, jnp.float32)
        for k in range(srow.shape[0] // LANES):
            row_k = (lax.broadcasted_iota(jnp.int32, (gsend.shape[0], n_bf), 0) == k).astype(jnp.float32)
            total = total + mm(row_k, srow[k * LANES:(k + 1) * LANES, :], 1, 1)
        gsend[...] = total
        grecv[me] = total
        for r in ORDER:
            g_copy(peer_orb(r), me).start()

    def coulomb():
        for r in range(1, n_orb):
            g_copy(me, peer_orb(r)).wait_recv()
        gam = grecv[0]
        for src in range(1, n_orb):
            gam = gam + grecv[src]
        for k in range(srow.shape[0] // LANES):
            row_k = (lax.broadcasted_iota(jnp.int32, (gsend.shape[0], n_bf), 0) == k).astype(jnp.float32)
            gbc[k * LANES:(k + 1) * LANES, :] = mm(gam, row_k, 0, 0)

        def body(m, carry):
            jrows[pl.ds(m, 1), 0:n_bf] = jnp.sum(bv[m] * gbc[0:q_loc, :], axis=0, keepdims=True)
            return carry

        lax.fori_loop(0, row_blk, body, 0)
        jpad = jrows[...]
        for a in range(n_aux):
            piece = jpad if a == 0 else pltpu.roll(jpad, 2 * LANES - a * n_cols, 1)
            jsend[a] = piece[:, 0:LANES]
        jrecv[my] = jsend[my]
        for r in range(1, n_aux):
            j_copy(lax.rem(my + r, n_aux), my).start()

    def collect(g):
        m0, mg, base = groups[g]
        for r in range(1, n_orb):
            t_copy(g, me, peer_orb(r)).wait_recv()
        for src in range(n_orb):
            for s in range(slots):
                xa[src * row_pad + m0:src * row_pad + m0 + mg, s * LANES:(s + 1) * LANES] = recv[src, base + s * mg:base + (s + 1) * mg, :]

    def collect_left():
        for r in range(1, n_orb):
            l_copy(me, peer_orb(r)).wait_recv()
        for src in range(n_orb):
            for s in range(n_ex):
                cols = slice((slots + s) * LANES, (slots + s + 1) * LANES)
                xa[src * row_pad:src * row_pad + whole, cols] = ex_recv[src, s * whole:(s + 1) * whole, :]
                at = n_ex * whole + s * rest
                xa[src * row_pad + whole:src * row_pad + row_blk, cols] = ex_recv[src, at:at + rest, :]

    for g in range(3):
        t_rows(g)
        if g == 0:
            pl.semaphore_wait(barrier, n_dev - 1)
        t_send(g)
    for g in range(3, n_groups):
        load_list[g].wait()
    load_list = load_list[:3] + [Loaded()] * (n_groups - 3)
    gamma_part()
    for g in range(3, n_groups):
        t_rows(g)
        t_send(g)
    left_rows()
    for r in ORDER:
        l_copy(peer_orb(r), me).start()
    ex_recv[me] = ex_send[me]
    xa[...] = jnp.zeros(xa.shape, jnp.float32)
    coulomb()
    for g in range(n_groups):
        collect(g)
    step_k = 4 * LANES
    kacc[...] = mm(xa[:, 0:step_k], xa[:, 0:step_k], 1, 1)
    for c0 in range(step_k, slots * LANES, step_k):
        part = xa[:, c0:c0 + step_k]
        kacc[...] += mm(part, part, 1, 1)
    collect_left()
    part = xa[:, slots * LANES:]
    kacc[...] += mm(part, part, 1, 1)

    half = row_pad // 2
    low_half = lax.broadcasted_iota(jnp.int32, (half, LANES), 1) < LANES // 2
    for orb in range(n_orb):
        for ctile in range(n_aux // 2):
            blk = kacc[orb * row_pad:(orb + 1) * row_pad, ctile * LANES:(ctile + 1) * LANES]
            top, bot = blk[0:half], blk[half:]
            ksend[2 * ctile * n_orb + orb] = jnp.where(low_half, top, pltpu.roll(bot, LANES // 2, 1))
            ksend[(2 * ctile + 1) * n_orb + orb] = jnp.where(low_half, pltpu.roll(top, LANES // 2, 1), bot)
    dev = my * n_orb + me
    krecv[dev] = ksend[dev]

    def k_send(step, carry):
        k_copy(lax.rem(me + lax.rem(step, n_orb), n_orb), lax.rem(my + step // n_orb, n_aux), dev).start()
        return carry

    lax.fori_loop(1, n_dev, k_send, 0)
    for r in range(1, n_aux):
        j_copy(my, lax.rem(my + r, n_aux)).wait_recv()
    jsum = jrecv[0]
    for src in range(1, n_aux):
        jsum = jsum + jrecv[src]

    def k_wait(step, carry):
        src = lax.rem(my + step // n_orb, n_aux) * n_orb + lax.rem(me + lax.rem(step, n_orb), n_orb)
        k_copy(me, my, src).wait_recv()
        return carry

    lax.fori_loop(1, n_dev, k_wait, 0)
    ksum = krecv[0]
    for src in range(1, n_dev):
        ksum = ksum + krecv[src]
    kblk = jnp.concatenate([ksum, pltpu.roll(ksum, LANES // 2, 1)], axis=0)
    pad_cols = row_pad - row_blk
    kcols = jnp.where(lax.broadcasted_iota(jnp.int32, (row_pad, LANES), 1) < row_blk, kblk, pltpu.roll(kblk, LANES - pad_cols, 1))
    out = 2.0 * jsum - kcols
    out_ref[...] = out[0:row_blk, 0:n_cols]

    for g in range(n_groups):
        for r in range(1, n_orb):
            t_copy(g, peer_orb(r), me).wait_send()
    for r in range(1, n_orb):
        l_copy(peer_orb(r), me).wait_send()
        g_copy(peer_orb(r), me).wait_send()
    for r in range(1, n_aux):
        j_copy(lax.rem(my + r, n_aux), my).wait_send()

    def k_drain(step, carry):
        k_copy(lax.rem(me + lax.rem(step, n_orb), n_orb), lax.rem(my + step // n_orb, n_aux), dev).wait_send()
        return carry

    lax.fori_loop(1, n_dev, k_drain, 0)


def solution(mesh):
    n_orb = mesh.shape['orb']
    n_aux = mesh.shape['aux']

    def local_fock(fit_loc, orbitals):
        q_loc, row_blk, n_bf = fit_loc.shape
        n_occ = orbitals.shape[1]
        n_cols = n_bf // n_aux
        row_pad = rup(row_blk, SUBL)
        occ_each = n_occ // n_orb
        q_main = q_loc // LANES * LANES
        n_tiles = q_main // LANES
        slots = n_tiles * occ_each
        whole = row_blk // SUBL * SUBL
        left_pad = rup(q_loc - q_main, SUBL)
        fold = LANES // left_pad
        pairs = occ_each // fold
        n_ex = pairs + 1
        extra = n_occ - n_orb * occ_each
        groups, base = [], 0
        for m0, mg in ((whole, 2), (whole + 2, row_blk - whole - 2)) + tuple((m0, SUBL) for m0 in range(0, whole, SUBL)):
            groups.append((m0, mg, base))
            base += slots * mg
            assert slots * mg % SUBL == 0
        assert n_orb == 2 * n_aux and n_cols == 2 * row_blk and occ_each % fold == 0 and occ_each < SUBL
        assert 0 < extra <= fold and (n_tiles + 1) * extra <= n_orb + 1 and row_pad * n_orb == 2 * LANES
        dims = (n_orb, n_aux, q_loc, row_blk, n_bf, n_occ, row_pad, occ_each, tuple(groups), q_main, left_pad, fold, n_cols)
        n_dev = n_orb * n_aux
        n_groups = len(groups)
        ex_rows = n_ex * whole + rup(n_ex * (row_blk - whole), SUBL)
        q_lanes = rup(q_loc, LANES)
        f32 = jnp.float32
        dma = pltpu.SemaphoreType.DMA
        scratch = [
            pltpu.VMEM((row_blk, q_loc, n_bf), f32),
            pltpu.VMEM((n_occ, n_bf), f32),
            pltpu.VMEM((n_orb * SUBL, n_bf), f32),
            pltpu.VMEM((fold * rup(pairs * n_orb + 1, SUBL), n_bf), f32),
            pltpu.VMEM((row_blk, n_bf), f32),
            pltpu.VMEM((n_orb, base, LANES), f32),
            pltpu.VMEM((n_orb, base, LANES), f32),
            pltpu.VMEM((n_orb, ex_rows, LANES), f32),
            pltpu.VMEM((n_orb, ex_rows, LANES), f32),
            pltpu.VMEM((n_orb * row_pad, (slots + n_ex) * LANES), f32),
            pltpu.VMEM((n_orb * row_pad, n_orb * row_pad), f32),
            pltpu.VMEM((q_lanes, n_bf), f32),
            pltpu.VMEM((SUBL, LANES), f32),
            pltpu.VMEM((n_orb, SUBL, LANES), f32),
            pltpu.VMEM((q_lanes, n_bf), f32),
            pltpu.VMEM((row_pad, 2 * LANES), f32),
            pltpu.VMEM((n_aux, row_pad, LANES), f32),
            pltpu.VMEM((n_aux, row_pad, LANES), f32),
            pltpu.VMEM((n_dev, row_pad // 2, LANES), f32),
            pltpu.VMEM((n_dev, row_pad // 2, LANES), f32),
            dma((n_groups + 1,)), dma((n_groups, n_orb)), dma((n_groups, n_orb)), dma((n_orb,)), dma((n_orb,)),
            dma((n_orb,)), dma((n_orb,)), dma((n_aux,)), dma((n_aux,)), dma((n_dev,)), dma((n_dev,)),
        ]
        return pl.pallas_call(
            functools.partial(fock_kernel, dims),
            out_shape=jax.ShapeDtypeStruct((row_blk, n_cols), f32),
            in_specs=[pl.BlockSpec(memory_space=pl.ANY), pl.BlockSpec(memory_space=pl.ANY)],
            out_specs=pl.BlockSpec(memory_space=pltpu.VMEM),
            scratch_shapes=scratch,
            compiler_params=pltpu.CompilerParams(collective_id=0, has_side_effects=True, vmem_limit_bytes=56 * 1024 * 1024),
            name='fock_build',
        )(jnp.transpose(fit_loc, (1, 0, 2)), orbitals.T)

    spec_fit = P(('sys', 'aux'), 'orb', None)
    spec_orbitals = P('sys', None)
    spec_out = P(('sys', 'orb'), 'aux')
    return jax.shard_map(local_fock, mesh=mesh, in_specs=(spec_fit, spec_orbitals), out_specs=spec_out, check_vma=False)
```

time: 266 us -> 47.8 us (0.18)
  the two profiles are of different devices: /device:TPU:96 before, /device:TPU:97 now
where the time goes in v2:
time: 47.8 us; the launch traced here: 47.6 us
  Pallas kernels  46.3 us (97%)
  local copies, waits for them, and re-layouts  1.32 us (3%)
    pallas_call x1, Pallas kernels, local_fock(): pl.pallas_call(functools.partial(fock_kernel, dims), out_shape=jax.ShapeD...  46.3 us
    unnamed x1, local copies, waits for them, and re-layouts  1.32 us

profile of v2, /device:TPU:97, one launch (start us, length us, event | category | flops | bytes accessed | tf_op | source)
XLA Modules:
  0.0 47.6 jit_solution(14459626538965912214)
XLA Ops:
  0.0 46.3 %fock_build.1 = f32[30,60]{1,0:T(8,128)} custom-call(f32[30,290,240]{2,1,0:T(8,128)} %bitcast.2, f32[50,240]{1,0:T(8,128)} %bitcast.3), custom_call_target="tpu_custom_call" | custom-call | tf_op jit(solution)/shard_map/fock_build/pallas_call | solution.py:360
  46.3 1.3 %copy.4 = f32[30,60]{1,0:T(8,128)} copy(f32[30,60]{1,0:T(8,128)} %fock_build.1) | data formatting | bytes 14400

commit v3 on v2

--- a/solution.py
+++ b/solution.py
@@ -13,6 +13,7 @@
 
 
 ORDER = (4, 2, 6, 5, 3, 7, 1)
+T_STEP = 2
 
 
 def mm(lhs, rhs, lhs_dim, rhs_dim):
@@ -28,7 +29,7 @@
         pass
 
 
-def fock_kernel(dims, fit_ref, occ_ref, out_ref, bv, ct, ctp, ctl, dens, recv, send, ex_recv, ex_send, xa, kacc,
+def fock_kernel(dims, fit_ref, occ_ref, out_ref, bv, ct, ctn, dens, recv, send, ex_recv, ex_send, xa, kacc,
                 srow, gsend, grecv, gbc, jrows, jsend, jrecv, ksend, krecv,
                 load_sem, t_ss, t_rs, l_ss, l_rs, g_ss, g_rs, j_ss, j_rs, k_ss, k_rs):
     (n_orb, n_aux, q_loc, row_blk, n_bf, n_occ, row_pad, occ_each, groups, q_main, left_pad, fold, n_cols) = dims
@@ -55,29 +56,24 @@
 
     barrier = pltpu.get_barrier_semaphore()
 
-    def greet(step, carry):
-        pl.semaphore_signal(barrier, inc=1, device_id={'orb': lax.rem(me + lax.rem(step, n_orb), n_orb), 'aux': lax.rem(my + step // n_orb, n_aux)}, device_id_type=MESH_ID)
-        return carry
-
-    lax.fori_loop(1, n_dev, greet, 0)
+    for r in range(1, n_orb):
+        pl.semaphore_signal(barrier, inc=1, device_id={'orb': peer_orb(r)}, device_id_type=MESH_ID)
+    for r in range(1, n_aux):
+        pl.semaphore_signal(barrier, inc=1, device_id={'aux': lax.rem(my + r, n_aux)}, device_id_type=MESH_ID)
     ex_send[...] = jnp.zeros(ex_send.shape, jnp.float32)
 
     occ_load.wait()
     occ_t = ct[...]
-
-    def rows_of_ct(which):
-        return mm(which.astype(jnp.float32), occ_t, 1, 0)
-
-    row = lax.broadcasted_iota(jnp.int32, (n_orb * SUBL, n_occ), 0)
-    col = lax.broadcasted_iota(jnp.int32, (n_orb * SUBL, n_occ), 1)
-    in_blk = row % SUBL
-    ctp[...] = rows_of_ct(((in_blk < occ_each) & (col == row // SUBL * occ_each + in_blk))
-                          | ((in_blk == occ_each) & (col == n_orb * occ_each + row // SUBL % extra)))
-    rows_l = ctl.shape[0] // fold
-    row = lax.broadcasted_iota(jnp.int32, (rows_l, n_occ), 0)
-    col = lax.broadcasted_iota(jnp.int32, (rows_l, n_occ), 1)
-    for j in range(fold):
-        ctl[j * rows_l:(j + 1) * rows_l, :] = rows_of_ct((row <= pairs * n_orb) & (col == row * fold + j))
+    rows_l = rup(pairs * n_orb + 1, SUBL)
+    row = lax.broadcasted_iota(jnp.int32, (n_occ, LANES), 0)
+    col = lax.broadcasted_iota(jnp.int32, (n_occ, LANES), 1)
+    in_blk = col % SUBL
+    which = (((in_blk < occ_each) & (row == col // SUBL * occ_each + in_blk))
+             | ((in_blk == occ_each) & (row == n_orb * occ_each + col // SUBL % extra))) & (col < n_orb * SUBL)
+    ctn[:, 0:LANES] = mm(occ_t, which.astype(jnp.float32), 0, 0)
+    in_blk = col % rows_l
+    which = (in_blk <= pairs * n_orb) & (row == in_blk * fold + col // rows_l) & (col < fold * rows_l)
+    ctn[:, LANES:] = mm(occ_t, which.astype(jnp.float32), 0, 0)
     pick = lax.broadcasted_iota(jnp.int32, (row_blk, n_bf), 0)
     pick_col = lax.broadcasted_iota(jnp.int32, (row_blk, n_bf), 1)
     own = mm((pick + me * row_blk == pick_col).astype(jnp.float32), occ_t, 1, 1)
@@ -120,8 +116,10 @@
         tail = m0 >= whole
         load_list[g].wait()
 
-        def step(m, carry):
-            block = mm(ctp[...], bv[m, 0:q_main, :], 1, 1)
+        def rows_of(m):
+            return [bv[m, 0:q_main, :], bv[m, q_main:q_loc, :], jnp.zeros((left_pad - q_left, n_bf), jnp.float32)]
+
+        def put(m, block, left):
             for d in range(n_orb):
                 for t in range(n_tiles):
                     piece = block[d * SUBL:d * SUBL + occ_each, t * LANES:(t + 1) * LANES]
@@ -129,35 +127,33 @@
                     if d // extra == t:
                         at = d * SUBL + occ_each
                         ex_send[d, pl.ds(ex_row(pairs, m, tail), 1), :] = block[at:at + 1, t * LANES:(t + 1) * LANES]
+            total = left[0:rows_l]
+            for j in range(1, fold):
+                total = total + pltpu.roll(left[j * rows_l:(j + 1) * rows_l], j * left_pad, 1)
+            for d in range(n_orb):
+                for u in range(pairs):
+                    ex_send[d, pl.ds(ex_row(u, m, tail), 1), :] = total[d * pairs + u:d * pairs + u + 1]
+            d = n_tiles * extra
+            ex_send[d, pl.ds(ex_row(pairs, m, tail), 1), :] = total[n_orb * pairs:n_orb * pairs + 1]
+
+        def step(k, carry):
+            m = m0 + k * T_STEP
+            rows = jnp.concatenate(sum([rows_of(m + j) for j in range(T_STEP)], []), axis=0)
+            block = mm(rows, ctn[...], 1, 0)
+            for j in range(T_STEP):
+                at = j * (q_main + left_pad)
+                left = block[at + q_main:at + q_main + left_pad, LANES:]
+                left = jnp.concatenate([left, jnp.zeros((LANES - left_pad, LANES), jnp.float32)], axis=0)
+                put(m + j, block[at:at + q_main, 0:LANES].T, left.T)
             return carry
 
-        lax.fori_loop(m0, m0 + mg, step, 0)
+        lax.fori_loop(0, mg // T_STEP, step, 0)
 
     def t_send(g):
         for r in ORDER:
             t_copy(g, peer_orb(r), me).start()
         m0, mg, base = groups[g]
         recv[me, base:base + slots * mg, :] = send[me, base:base + slots * mg, :]
-
-    def left_rows():
-        for m0, m1 in ((0, whole), (whole, row_blk)):
-            tail = m0 >= whole
-
-            def step(m, carry):
-                rows = jnp.concatenate([bv[m, q_main:q_loc, :], jnp.zeros((left_pad - q_left, n_bf), jnp.float32)], axis=0)
-                block = mm(ctl[...], rows, 1, 1)
-                block = jnp.concatenate([block, jnp.zeros((fold * rows_l, LANES - left_pad), jnp.float32)], axis=1)
-                total = block[0:rows_l]
-                for j in range(1, fold):
-                    total = total + pltpu.roll(block[j * rows_l:(j + 1) * rows_l], j * left_pad, 1)
-                for d in range(n_orb):
-                    for u in range(pairs):
-                        ex_send[d, pl.ds(ex_row(u, m, tail), 1), :] = total[d * pairs + u:d * pairs + u + 1]
-                d = n_tiles * extra
-                ex_send[d, pl.ds(ex_row(pairs, m, tail), 1), :] = total[n_orb * pairs:n_orb * pairs + 1]
-                return carry
-
-            lax.fori_loop(m0, m1, step, 0)
 
     def gamma_part():
         q_step = 5 * SUBL
@@ -218,11 +214,13 @@
                 at = n_ex * whole + s * rest
                 xa[src * row_pad + whole:src * row_pad + row_blk, cols] = ex_recv[src, at:at + rest, :]
 
-    for g in range(3):
-        t_rows(g)
-        if g == 0:
-            pl.semaphore_wait(barrier, n_dev - 1)
-        t_send(g)
+    t_rows(0)
+    t_rows(1)
+    pl.semaphore_wait(barrier, n_orb - 1 + n_aux - 1)
+    t_send(0)
+    t_send(1)
+    t_rows(2)
+    t_send(2)
     for g in range(3, n_groups):
         load_list[g].wait()
     load_list = load_list[:3] + [Loaded()] * (n_groups - 3)
@@ -230,7 +228,6 @@
     for g in range(3, n_groups):
         t_rows(g)
         t_send(g)
-    left_rows()
     for r in ORDER:
         l_copy(peer_orb(r), me).start()
     ex_recv[me] = ex_send[me]
@@ -258,23 +255,24 @@
     dev = my * n_orb + me
     krecv[dev] = ksend[dev]
 
-    def k_send(step, carry):
-        k_copy(lax.rem(me + lax.rem(step, n_orb), n_orb), lax.rem(my + step // n_orb, n_aux), dev).start()
-        return carry
-
-    lax.fori_loop(1, n_dev, k_send, 0)
+    def hops(step, ring):
+        return min(step, ring - step)
+
+    steps = sorted(range(1, n_dev), key=lambda k: -(hops((k % n_orb + 1) // 2, n_orb // 2) + hops(k // n_orb, n_aux)))
+
+    def k_out(step):
+        return k_copy(peer_orb(step % n_orb), lax.rem(my + step // n_orb, n_aux), dev)
+
+    for step in steps:
+        k_out(step).start()
     for r in range(1, n_aux):
         j_copy(my, lax.rem(my + r, n_aux)).wait_recv()
     jsum = jrecv[0]
     for src in range(1, n_aux):
         jsum = jsum + jrecv[src]
 
-    def k_wait(step, carry):
-        src = lax.rem(my + step // n_orb, n_aux) * n_orb + lax.rem(me + lax.rem(step, n_orb), n_orb)
-        k_copy(me, my, src).wait_recv()
-        return carry
-
-    lax.fori_loop(1, n_dev, k_wait, 0)
+    for step in reversed(steps):
+        k_copy(me, my, lax.rem(my + step // n_orb, n_aux) * n_orb + peer_orb(step % n_orb)).wait_recv()
     ksum = krecv[0]
     for src in range(1, n_dev):
         ksum = ksum + krecv[src]
@@ -293,11 +291,8 @@
     for r in range(1, n_aux):
         j_copy(lax.rem(my + r, n_aux), my).wait_send()
 
-    def k_drain(step, carry):
-        k_copy(lax.rem(me + lax.rem(step, n_orb), n_orb), lax.rem(my + step // n_orb, n_aux), dev).wait_send()
-        return carry
-
-    lax.fori_loop(1, n_dev, k_drain, 0)
+    for step in steps:
+        k_out(step).wait_send()
 
 
 def solution(mesh):
@@ -336,8 +331,7 @@
         scratch = [
             pltpu.VMEM((row_blk, q_loc, n_bf), f32),
             pltpu.VMEM((n_occ, n_bf), f32),
-            pltpu.VMEM((n_orb * SUBL, n_bf), f32),
-            pltpu.VMEM((fold * rup(pairs * n_orb + 1, SUBL), n_bf), f32),
+            pltpu.VMEM((n_bf, 2 * LANES), f32),
             pltpu.VMEM((row_blk, n_bf), f32),
             pltpu.VMEM((n_orb, base, LANES), f32),
             pltpu.VMEM((n_orb, base, LANES), f32),

time: 47.8 us -> 43 us (0.90)
  Pallas kernels: 46.3 us -> 41.5 us
    pallas_call x1, Pallas kernels: 46.3 us -> 41.5 us  [local_fock(): pl.pallas_call(functools.partial(fock_kernel, dims), out_shape=jax.ShapeD...]
where the time goes in v3:
time: 43 us; the launch traced here: 42.8 us
  Pallas kernels  41.5 us (97%)
  local copies, waits for them, and re-layouts  1.32 us (3%)
    pallas_call x1, Pallas kernels, local_fock(): pl.pallas_call(functools.partial(fock_kernel, dims), out_shape=jax.ShapeD...  41.5 us
    unnamed x1, local copies, waits for them, and re-layouts  1.32 us

profile of v3, /device:TPU:97, one launch (start us, length us, event | category | flops | bytes accessed | tf_op | source)
XLA Modules:
  0.0 42.8 jit_solution(10701438564319668071)
XLA Ops:
  0.0 41.5 %fock_build.1 = f32[30,60]{1,0:T(8,128)} custom-call(f32[30,290,240]{2,1,0:T(8,128)} %bitcast.2, f32[50,240]{1,0:T(8,128)} %bitcast.3), custom_call_target="tpu_custom_call" | custom-call | tf_op jit(solution)/shard_map/fock_build/pallas_call | solution.py:354
  41.5 1.3 %copy.4 = f32[30,60]{1,0:T(8,128)} copy(f32[30,60]{1,0:T(8,128)} %fock_build.1) | data formatting | bytes 14400

commit v4 on v3

--- a/solution.py
+++ b/solution.py
@@ -13,7 +13,8 @@
 
 
 ORDER = (4, 2, 6, 5, 3, 7, 1)
-T_STEP = 2
+SMALL_STEP = 6
+WHOLE_STEP = 8
 
 
 def mm(lhs, rhs, lhs_dim, rhs_dim):
@@ -22,23 +23,17 @@
 
 def rup(value, unit):
     return -(-value // unit) * unit
-
-
-class Loaded:
-    def wait(self):
-        pass
 
 
 def fock_kernel(dims, fit_ref, occ_ref, out_ref, bv, ct, ctn, dens, recv, send, ex_recv, ex_send, xa, kacc,
                 srow, gsend, grecv, gbc, jrows, jsend, jrecv, ksend, krecv,
                 load_sem, t_ss, t_rs, l_ss, l_rs, g_ss, g_rs, j_ss, j_rs, k_ss, k_rs):
-    (n_orb, n_aux, q_loc, row_blk, n_bf, n_occ, row_pad, occ_each, groups, q_main, left_pad, fold, n_cols) = dims
+    (n_orb, n_aux, q_loc, row_blk, n_bf, n_occ, row_pad, occ_each, q_main, left_pad, fold, n_cols) = dims
     me = lax.axis_index('orb')
     my = lax.axis_index('aux')
     n_dev = n_orb * n_aux
     n_tiles = q_main // LANES
     slots = n_tiles * occ_each
-    n_groups = len(groups)
     q_left = q_loc - q_main
     whole = row_blk // SUBL * SUBL
     rest = row_blk - whole
@@ -48,11 +43,26 @@
     def peer_orb(step):
         return lax.rem(me + step, n_orb)
 
+    n_small = 1
+    n_whole = whole // SUBL
+    n_groups = n_small + n_whole
+    small_rows, whole_rows = slots * rest, slots * SUBL
+
+    def load(first, count, sem):
+        return pltpu.make_async_copy(fit_ref.at[pl.ds(first, count)], bv.at[pl.ds(first, count)], load_sem.at[sem])
+
+    def small_load(k):
+        return load(whole, rest, k)
+
+    def whole_load(k):
+        return load(k * SUBL, SUBL, n_small + k)
+
     occ_load = pltpu.make_async_copy(occ_ref, ct, load_sem.at[n_groups])
     occ_load.start()
-    load_list = [pltpu.make_async_copy(fit_ref.at[pl.ds(m0, mg)], bv.at[pl.ds(m0, mg)], load_sem.at[g]) for g, (m0, mg, base) in enumerate(groups)]
-    for cp in load_list:
-        cp.start()
+    for k in range(n_small):
+        small_load(k).start()
+    for k in range(n_whole):
+        whole_load(k).start()
 
     barrier = pltpu.get_barrier_semaphore()
 
@@ -74,21 +84,23 @@
     in_blk = col % rows_l
     which = (in_blk <= pairs * n_orb) & (row == in_blk * fold + col // rows_l) & (col < fold * rows_l)
     ctn[:, LANES:] = mm(occ_t, which.astype(jnp.float32), 0, 0)
-    pick = lax.broadcasted_iota(jnp.int32, (row_blk, n_bf), 0)
-    pick_col = lax.broadcasted_iota(jnp.int32, (row_blk, n_bf), 1)
-    own = mm((pick + me * row_blk == pick_col).astype(jnp.float32), occ_t, 1, 1)
-    dens[...] = mm(own, occ_t, 1, 0)
-
-    def t_copy(g, dst, src_dev):
-        m0, mg, base = groups[g]
+    def t_copy(is_small, k, dst, src_dev):
+        rows = pl.ds(pl.multiple_of(k * small_rows, SUBL), small_rows) if is_small else pl.ds(pl.multiple_of(n_small * small_rows + k * whole_rows, SUBL), whole_rows)
+        g = k if is_small else n_small + k
         return pltpu.make_async_remote_copy(
-            src_ref=send.at[dst, pl.ds(base, slots * mg)], dst_ref=recv.at[src_dev, pl.ds(base, slots * mg)],
+            src_ref=send.at[dst, rows], dst_ref=recv.at[src_dev, rows],
             send_sem=t_ss.at[g, dst], recv_sem=t_rs.at[g, src_dev], device_id={'orb': dst}, device_id_type=MESH_ID)
 
-    def l_copy(dst, src_dev):
+    t_groups = [(True, k) for k in range(n_small)] + [(False, k) for k in range(n_whole)]
+
+    def l_copy(part, dst, src_dev):
+        rows = pl.ds(0, last_row) if part == 0 else pl.ds(last_row, ex_send.shape[1] - last_row)
         return pltpu.make_async_remote_copy(
-            src_ref=ex_send.at[dst], dst_ref=ex_recv.at[src_dev], send_sem=l_ss.at[dst], recv_sem=l_rs.at[src_dev],
+            src_ref=ex_send.at[dst, rows], dst_ref=ex_recv.at[src_dev, rows], send_sem=l_ss.at[part, dst], recv_sem=l_rs.at[part, src_dev],
             device_id={'orb': dst}, device_id_type=MESH_ID)
+
+    def if_last(dst, act):
+        pl.when(dst <= n_tiles * extra)(act)
 
     def g_copy(dst, src_dev):
         return pltpu.make_async_remote_copy(
@@ -107,26 +119,25 @@
             device_id={'orb': orb, 'aux': aux}, device_id_type=MESH_ID)
 
     def ex_row(slot, m, tail):
-        return (n_ex * whole + slot * rest + m - whole) if tail else (slot * whole + m)
-
-    n_ex = pairs + 1
-
-    def t_rows(g):
-        m0, mg, base = groups[g]
-        tail = m0 >= whole
-        load_list[g].wait()
+        if slot == pairs:
+            return last_row + m
+        return (pairs * whole + slot * rest + m - whole) if tail else (slot * whole + m)
+
+    last_row = rup(pairs * row_blk, SUBL)
+
+    def t_part(count, m, at, mg, tail):
 
         def rows_of(m):
             return [bv[m, 0:q_main, :], bv[m, q_main:q_loc, :], jnp.zeros((left_pad - q_left, n_bf), jnp.float32)]
 
-        def put(m, block, left):
+        def put(m, at_m, block, left):
             for d in range(n_orb):
                 for t in range(n_tiles):
                     piece = block[d * SUBL:d * SUBL + occ_each, t * LANES:(t + 1) * LANES]
-                    send[d, pl.ds(base + t * occ_each * mg + m - m0, occ_each, stride=mg), :] = piece
+                    send[d, pl.ds(at_m + t * occ_each * mg, occ_each, stride=mg), :] = piece
                     if d // extra == t:
-                        at = d * SUBL + occ_each
-                        ex_send[d, pl.ds(ex_row(pairs, m, tail), 1), :] = block[at:at + 1, t * LANES:(t + 1) * LANES]
+                        pick = d * SUBL + occ_each
+                        ex_send[d, pl.ds(ex_row(pairs, m, tail), 1), :] = block[pick:pick + 1, t * LANES:(t + 1) * LANES]
             total = left[0:rows_l]
             for j in range(1, fold):
                 total = total + pltpu.roll(left[j * rows_l:(j + 1) * rows_l], j * left_pad, 1)
@@ -136,26 +147,52 @@
             d = n_tiles * extra
             ex_send[d, pl.ds(ex_row(pairs, m, tail), 1), :] = total[n_orb * pairs:n_orb * pairs + 1]
 
-        def step(k, carry):
-            m = m0 + k * T_STEP
-            rows = jnp.concatenate(sum([rows_of(m + j) for j in range(T_STEP)], []), axis=0)
-            block = mm(rows, ctn[...], 1, 0)
-            for j in range(T_STEP):
-                at = j * (q_main + left_pad)
-                left = block[at + q_main:at + q_main + left_pad, LANES:]
-                left = jnp.concatenate([left, jnp.zeros((LANES - left_pad, LANES), jnp.float32)], axis=0)
-                put(m + j, block[at:at + q_main, 0:LANES].T, left.T)
+        rows = jnp.concatenate(sum([rows_of(m + j) for j in range(count)], []), axis=0)
+        block = mm(rows, ctn[...], 1, 0)
+        for j in range(count):
+            top = j * (q_main + left_pad)
+            left = block[top + q_main:top + q_main + left_pad, LANES:]
+            left = jnp.concatenate([left, jnp.zeros((LANES - left_pad, LANES), jnp.float32)], axis=0)
+            put(m + j, at + j, block[top:top + q_main, 0:LANES].T, left.T)
+
+    def t_send(is_small, k):
+        for r in ORDER:
+            t_copy(is_small, k, peer_orb(r), me).start()
+
+    def t_small():
+        small_load(0).wait()
+
+        def step(j, carry):
+            t_part(SMALL_STEP, whole + j * SMALL_STEP, j * SMALL_STEP, rest, True)
             return carry
 
-        lax.fori_loop(0, mg // T_STEP, step, 0)
-
-    def t_send(g):
-        for r in ORDER:
-            t_copy(g, peer_orb(r), me).start()
-        m0, mg, base = groups[g]
-        recv[me, base:base + slots * mg, :] = send[me, base:base + slots * mg, :]
+        lax.fori_loop(0, rest // SMALL_STEP, step, 0)
+        pl.semaphore_wait(barrier, n_orb - 1 + n_aux - 1)
+        t_send(True, 0)
+
+    def t_whole(k, carry):
+        @pl.when(k < n_whole - 1)
+        def _():
+            whole_load(k).wait()
+
+        def step(j, inner):
+            t_part(WHOLE_STEP, k * SUBL + j * WHOLE_STEP, n_small * small_rows + k * whole_rows + j * WHOLE_STEP, SUBL, False)
+            return inner
+
+        lax.fori_loop(0, SUBL // WHOLE_STEP, step, 0)
+        t_send(False, k)
+
+        @pl.when(k == n_whole - 2)
+        def _():
+            gamma_part()
+        return carry
 
     def gamma_part():
+        whole_load(n_whole - 1).wait()
+        pick = lax.broadcasted_iota(jnp.int32, (row_blk, n_bf), 0)
+        pick_col = lax.broadcasted_iota(jnp.int32, (row_blk, n_bf), 1)
+        own = mm((pick + me * row_blk == pick_col).astype(jnp.float32), occ_t, 1, 1)
+        dens[...] = mm(own, occ_t, 1, 0)
         q_step = 5 * SUBL
         for q0 in range(0, q_loc, q_step):
             n_q = min(q_step, q_loc - q0)
@@ -196,53 +233,70 @@
         for r in range(1, n_aux):
             j_copy(lax.rem(my + r, n_aux), my).start()
 
-    def collect(g):
-        m0, mg, base = groups[g]
+    def collect():
+        for is_small, k in t_groups:
+            for r in range(1, n_orb):
+                t_copy(is_small, k, me, peer_orb(r)).wait_recv()
+        recv[me] = send[me]
+
+        def small(src, carry):
+            for s in range(slots):
+                xa[src, whole:row_blk, s * LANES:(s + 1) * LANES] = recv[src, s * rest:(s + 1) * rest, :]
+            return carry
+
+        lax.fori_loop(0, n_orb, small, 0)
+
+        def tiles(n, carry):
+            src, k = n // n_whole, lax.rem(n, n_whole)
+            for s in range(slots):
+                at = pl.multiple_of(n_small * small_rows + k * whole_rows + s * SUBL, SUBL)
+                xa[src, pl.ds(pl.multiple_of(k * SUBL, SUBL), SUBL), s * LANES:(s + 1) * LANES] = recv[src, pl.ds(at, SUBL), :]
+            return carry
+
+        lax.fori_loop(0, n_orb * n_whole, tiles, 0)
+
+    def collect_left(part):
         for r in range(1, n_orb):
-            t_copy(g, me, peer_orb(r)).wait_recv()
+            if part == 0:
+                l_copy(0, me, peer_orb(r)).wait_recv()
+            else:
+                if_last(me, l_copy(1, me, peer_orb(r)).wait_recv)
         for src in range(n_orb):
-            for s in range(slots):
-                xa[src * row_pad + m0:src * row_pad + m0 + mg, s * LANES:(s + 1) * LANES] = recv[src, base + s * mg:base + (s + 1) * mg, :]
-
-    def collect_left():
-        for r in range(1, n_orb):
-            l_copy(me, peer_orb(r)).wait_recv()
-        for src in range(n_orb):
-            for s in range(n_ex):
+            for s in range(pairs) if part == 0 else (pairs,):
                 cols = slice((slots + s) * LANES, (slots + s + 1) * LANES)
-                xa[src * row_pad:src * row_pad + whole, cols] = ex_recv[src, s * whole:(s + 1) * whole, :]
-                at = n_ex * whole + s * rest
-                xa[src * row_pad + whole:src * row_pad + row_blk, cols] = ex_recv[src, at:at + rest, :]
-
-    t_rows(0)
-    t_rows(1)
-    pl.semaphore_wait(barrier, n_orb - 1 + n_aux - 1)
-    t_send(0)
-    t_send(1)
-    t_rows(2)
-    t_send(2)
-    for g in range(3, n_groups):
-        load_list[g].wait()
-    load_list = load_list[:3] + [Loaded()] * (n_groups - 3)
-    gamma_part()
-    for g in range(3, n_groups):
-        t_rows(g)
-        t_send(g)
+                at = ex_row(s, 0, False)
+                xa[src, 0:whole, cols] = ex_recv[src, at:at + whole, :]
+                at = ex_row(s, whole, True)
+                xa[src, whole:row_blk, cols] = ex_recv[src, at:at + rest, :]
+
+    t_small()
+    lax.fori_loop(0, n_whole, t_whole, 0)
     for r in ORDER:
-        l_copy(peer_orb(r), me).start()
+        l_copy(0, peer_orb(r), me).start()
+    for r in ORDER:
+        if_last(peer_orb(r), l_copy(1, peer_orb(r), me).start)
     ex_recv[me] = ex_send[me]
     xa[...] = jnp.zeros(xa.shape, jnp.float32)
     coulomb()
-    for g in range(n_groups):
-        collect(g)
-    step_k = 4 * LANES
-    kacc[...] = mm(xa[:, 0:step_k], xa[:, 0:step_k], 1, 1)
-    for c0 in range(step_k, slots * LANES, step_k):
-        part = xa[:, c0:c0 + step_k]
+    collect()
+    kacc[...] = jnp.zeros(kacc.shape, jnp.float32)
+    depth = 2 * LANES
+    n_main = slots * LANES // depth
+
+    def k_step(k, carry):
+        @pl.when(k == n_main)
+        def _():
+            collect_left(0)
+
+        @pl.when(k == n_main + 1)
+        def _():
+            collect_left(1)
+
+        part = xa[:, :, pl.ds(pl.multiple_of(k * depth, depth), depth)].reshape(n_orb * row_pad, depth)
         kacc[...] += mm(part, part, 1, 1)
-    collect_left()
-    part = xa[:, slots * LANES:]
-    kacc[...] += mm(part, part, 1, 1)
+        return carry
+
+    lax.fori_loop(0, n_main + 2, k_step, 0)
 
     half = row_pad // 2
     low_half = lax.broadcasted_iota(jnp.int32, (half, LANES), 1) < LANES // 2
@@ -265,6 +319,15 @@
 
     for step in steps:
         k_out(step).start()
+    for is_small, k in t_groups:
+        for r in range(1, n_orb):
+            t_copy(is_small, k, peer_orb(r), me).wait_send()
+    for r in range(1, n_orb):
+        l_copy(0, peer_orb(r), me).wait_send()
+        if_last(peer_orb(r), l_copy(1, peer_orb(r), me).wait_send)
+        g_copy(peer_orb(r), me).wait_send()
+    for r in range(1, n_aux):
+        j_copy(lax.rem(my + r, n_aux), my).wait_send()
     for r in range(1, n_aux):
         j_copy(my, lax.rem(my + r, n_aux)).wait_recv()
     jsum = jrecv[0]
@@ -281,15 +344,6 @@
     kcols = jnp.where(lax.broadcasted_iota(jnp.int32, (row_pad, LANES), 1) < row_blk, kblk, pltpu.roll(kblk, LANES - pad_cols, 1))
     out = 2.0 * jsum - kcols
     out_ref[...] = out[0:row_blk, 0:n_cols]
-
-    for g in range(n_groups):
-        for r in range(1, n_orb):
-            t_copy(g, peer_orb(r), me).wait_send()
-    for r in range(1, n_orb):
-        l_copy(peer_orb(r), me).wait_send()
-        g_copy(peer_orb(r), me).wait_send()
-    for r in range(1, n_aux):
-        j_copy(lax.rem(my + r, n_aux), my).wait_send()
 
     for step in steps:
         k_out(step).wait_send()
@@ -312,19 +366,16 @@
         left_pad = rup(q_loc - q_main, SUBL)
         fold = LANES // left_pad
         pairs = occ_each // fold
-        n_ex = pairs + 1
         extra = n_occ - n_orb * occ_each
-        groups, base = [], 0
-        for m0, mg in ((whole, 2), (whole + 2, row_blk - whole - 2)) + tuple((m0, SUBL) for m0 in range(0, whole, SUBL)):
-            groups.append((m0, mg, base))
-            base += slots * mg
-            assert slots * mg % SUBL == 0
+        base = slots * row_blk
+        rest = row_blk - whole
         assert n_orb == 2 * n_aux and n_cols == 2 * row_blk and occ_each % fold == 0 and occ_each < SUBL
         assert 0 < extra <= fold and (n_tiles + 1) * extra <= n_orb + 1 and row_pad * n_orb == 2 * LANES
-        dims = (n_orb, n_aux, q_loc, row_blk, n_bf, n_occ, row_pad, occ_each, tuple(groups), q_main, left_pad, fold, n_cols)
+        dims = (n_orb, n_aux, q_loc, row_blk, n_bf, n_occ, row_pad, occ_each, q_main, left_pad, fold, n_cols)
         n_dev = n_orb * n_aux
-        n_groups = len(groups)
-        ex_rows = n_ex * whole + rup(n_ex * (row_blk - whole), SUBL)
+        n_groups = 1 + whole // SUBL
+        assert rest % SMALL_STEP == 0 and slots * rest % SUBL == 0 and slots % 2 == 0 and pairs == 2
+        ex_rows = rup(pairs * row_blk, SUBL) + rup(row_blk, SUBL)
         q_lanes = rup(q_loc, LANES)
         f32 = jnp.float32
         dma = pltpu.SemaphoreType.DMA
@@ -337,7 +388,7 @@
             pltpu.VMEM((n_orb, base, LANES), f32),
             pltpu.VMEM((n_orb, ex_rows, LANES), f32),
             pltpu.VMEM((n_orb, ex_rows, LANES), f32),
-            pltpu.VMEM((n_orb * row_pad, (slots + n_ex) * LANES), f32),
+            pltpu.VMEM((n_orb, row_pad, (slots + pairs + 2) * LANES), f32),
             pltpu.VMEM((n_orb * row_pad, n_orb * row_pad), f32),
             pltpu.VMEM((q_lanes, n_bf), f32),
             pltpu.VMEM((SUBL, LANES), f32),
@@ -348,13 +399,13 @@
             pltpu.VMEM((n_aux, row_pad, LANES), f32),
             pltpu.VMEM((n_dev, row_pad // 2, LANES), f32),
             pltpu.VMEM((n_dev, row_pad // 2, LANES), f32),
-            dma((n_groups + 1,)), dma((n_groups, n_orb)), dma((n_groups, n_orb)), dma((n_orb,)), dma((n_orb,)),
+            dma((n_groups + 1,)), dma((n_groups, n_orb)), dma((n_groups, n_orb)), dma((2, n_orb)), dma((2, n_orb)),
             dma((n_orb,)), dma((n_orb,)), dma((n_aux,)), dma((n_aux,)), dma((n_dev,)), dma((n_dev,)),
         ]
         return pl.pallas_call(
             functools.partial(fock_kernel, dims),
             out_shape=jax.ShapeDtypeStruct((row_blk, n_cols), f32),
-            in_specs=[pl.BlockSpec(memory_space=pl.ANY), pl.BlockSpec(memory_space=pl.ANY)],
+            in_specs=[pl.BlockSpec(memory_space=pltpu.HBM)] * 2,
             out_specs=pl.BlockSpec(memory_space=pltpu.VMEM),
             scratch_shapes=scratch,
             compiler_params=pltpu.CompilerParams(collective_id=0, has_side_effects=True, vmem_limit_bytes=56 * 1024 * 1024),

time: 43 us -> 41.8 us (0.972)
  Pallas kernels: 41.5 us -> 40.3 us
    pallas_call x1, Pallas kernels: 41.5 us -> 40.3 us  [local_fock(): pl.pallas_call(functools.partial(fock_kernel, dims), out_shape=jax.ShapeD...]
where the time goes in v4:
time: 41.8 us; the launch traced here: 41.6 us
  Pallas kernels  40.3 us (96%)
  local copies, waits for them, and re-layouts  1.32 us (3%)
    pallas_call x1, Pallas kernels, local_fock(): pl.pallas_call(functools.partial(fock_kernel, dims), out_shape=jax.ShapeD...  40.3 us
    unnamed x1, local copies, waits for them, and re-layouts  1.32 us

profile of v4, /device:TPU:97, one launch (start us, length us, event | category | flops | bytes accessed | tf_op | source)
XLA Modules:
  0.0 41.6 jit_solution(8587801368211386209)
XLA Ops:
  0.0 40.3 %fock_build.1 = f32[30,60]{1,0:T(8,128)} custom-call(f32[30,290,240]{2,1,0:T(8,128)} %bitcast.2, f32[50,240]{1,0:T(8,128)} %bitcast.3), custom_call_target="tpu_custom_call" | custom-call | tf_op jit(solution)/shard_map/fock_build/pallas_call | solution.py:405
  40.3 1.3 %copy.4 = f32[30,60]{1,0:T(8,128)} copy(f32[30,60]{1,0:T(8,128)} %fock_build.1) | data formatting | bytes 14400

commit v5 on v4

--- a/solution.py
+++ b/solution.py
@@ -234,26 +234,31 @@
             j_copy(lax.rem(my + r, n_aux), my).start()
 
     def collect():
-        for is_small, k in t_groups:
-            for r in range(1, n_orb):
-                t_copy(is_small, k, me, peer_orb(r)).wait_recv()
         recv[me] = send[me]
-
-        def small(src, carry):
+        for r in range(1, n_orb):
+            t_copy(True, 0, me, peer_orb(r)).wait_recv()
+
+        def last_rows(src, carry):
             for s in range(slots):
                 xa[src, whole:row_blk, s * LANES:(s + 1) * LANES] = recv[src, s * rest:(s + 1) * rest, :]
             return carry
 
-        lax.fori_loop(0, n_orb, small, 0)
-
-        def tiles(n, carry):
-            src, k = n // n_whole, lax.rem(n, n_whole)
-            for s in range(slots):
-                at = pl.multiple_of(n_small * small_rows + k * whole_rows + s * SUBL, SUBL)
-                xa[src, pl.ds(pl.multiple_of(k * SUBL, SUBL), SUBL), s * LANES:(s + 1) * LANES] = recv[src, pl.ds(at, SUBL), :]
+        lax.fori_loop(0, n_orb, last_rows, 0)
+
+        def one_whole(k, carry):
+            for r in range(1, n_orb):
+                t_copy(False, k, me, peer_orb(r)).wait_recv()
+
+            def tiles(src, inner):
+                for s in range(slots):
+                    at = pl.multiple_of(n_small * small_rows + k * whole_rows + s * SUBL, SUBL)
+                    xa[src, pl.ds(pl.multiple_of(k * SUBL, SUBL), SUBL), s * LANES:(s + 1) * LANES] = recv[src, pl.ds(at, SUBL), :]
+                return inner
+
+            lax.fori_loop(0, n_orb, tiles, 0)
             return carry
 
-        lax.fori_loop(0, n_orb * n_whole, tiles, 0)
+        lax.fori_loop(0, n_whole, one_whole, 0)
 
     def collect_left(part):
         for r in range(1, n_orb):
@@ -377,6 +382,7 @@
         assert rest % SMALL_STEP == 0 and slots * rest % SUBL == 0 and slots % 2 == 0 and pairs == 2
         ex_rows = rup(pairs * row_blk, SUBL) + rup(row_blk, SUBL)
         q_lanes = rup(q_loc, LANES)
+        g_rows = rup(q_lanes // LANES, 4)
         f32 = jnp.float32
         dma = pltpu.SemaphoreType.DMA
         scratch = [
@@ -391,8 +397,8 @@
             pltpu.VMEM((n_orb, row_pad, (slots + pairs + 2) * LANES), f32),
             pltpu.VMEM((n_orb * row_pad, n_orb * row_pad), f32),
             pltpu.VMEM((q_lanes, n_bf), f32),
-            pltpu.VMEM((SUBL, LANES), f32),
-            pltpu.VMEM((n_orb, SUBL, LANES), f32),
+            pltpu.VMEM((g_rows, LANES), f32),
+            pltpu.VMEM((n_orb, g_rows, LANES), f32),
             pltpu.VMEM((q_lanes, n_bf), f32),
             pltpu.VMEM((row_pad, 2 * LANES), f32),
             pltpu.VMEM((n_aux, row_pad, LANES), f32),
@@ -408,9 +414,9 @@
             in_specs=[pl.BlockSpec(memory_space=pltpu.HBM)] * 2,
             out_specs=pl.BlockSpec(memory_space=pltpu.VMEM),
             scratch_shapes=scratch,
-            compiler_params=pltpu.CompilerParams(collective_id=0, has_side_effects=True, vmem_limit_bytes=56 * 1024 * 1024),
+            compiler_params=pltpu.CompilerParams(collective_id=0, has_side_effects=True, vmem_limit_bytes=32 * 1024 * 1024),
             name='fock_build',
-        )(jnp.transpose(fit_loc, (1, 0, 2)), orbitals.T)
+        )(pltpu.with_memory_space_constraint(jnp.transpose(fit_loc, (1, 0, 2)), pltpu.HBM), pltpu.with_memory_space_constraint(orbitals.T, pltpu.HBM))
 
     spec_fit = P(('sys', 'aux'), 'orb', None)
     spec_orbitals = P('sys', None)

time: 41.8 us -> 39.9 us (0.955)
  Pallas kernels: 40.3 us -> 39.2 us
  local copies, waits for them, and re-layouts: 1.32 us -> 0.61 us
    pallas_call x1, Pallas kernels: 40.3 us -> 39.2 us  [local_fock(): pl.pallas_call(functools.partial(fock_kernel, dims), out_shape=jax.ShapeD...]
    unnamed x1, local copies, waits for them, and re-layouts: 1.32 us -> 0.61 us
where the time goes in v5:
time: 39.9 us; the launch traced here: 39.8 us
  Pallas kernels  39.2 us (98%)
  local copies, waits for them, and re-layouts  0.61 us (2%)
    pallas_call x1, Pallas kernels, local_fock(): pl.pallas_call(functools.partial(fock_kernel, dims), out_shape=jax.ShapeD...  39.2 us

profile of v5, /device:TPU:97, one launch (start us, length us, event | category | flops | bytes accessed | tf_op | source)
XLA Modules:
  0.0 39.8 jit_solution(2385381415633835194)
XLA Ops:
  0.0 39.2 %fock_build.1 = f32[30,60]{1,0:T(8,128)S(1)} custom-call(f32[30,290,240]{2,1,0:T(8,128)} %bitcast.2, f32[50,240]{1,0:T(8,128)} %bitcast.3), custom_call_target="tpu_custom_call" | custom-call | tf_op jit(solution)/shard_map/fock_build/pallas_call | solution.py:411
  39.2 0.6 %copy.4 = f32[30,60]{1,0:T(8,128)} copy(f32[30,60]{1,0:T(8,128)S(1)} %fock_build.1) | data formatting | bytes 14400

commit v6 on v5

--- a/solution.py
+++ b/solution.py
@@ -12,7 +12,7 @@
 SUBL = 8
 
 
-ORDER = (4, 2, 6, 5, 3, 7, 1)
+ORDER = ((2, 0), (2, 1), (1, 0), (3, 0), (1, 1), (3, 1), (0, 1))
 SMALL_STEP = 6
 WHOLE_STEP = 8
 
@@ -43,6 +43,13 @@
     def peer_orb(step):
         return lax.rem(me + step, n_orb)
 
+    chip, core = me // 2, lax.rem(me, 2)
+    n_chips = n_orb // 2
+
+    def peer_at(place):
+        ahead, flip = place
+        return lax.rem(chip + ahead, n_chips) * 2 + (1 - core if flip else core)
+
     n_small = 1
     n_whole = whole // SUBL
     n_groups = n_small + n_whole
@@ -61,8 +68,6 @@
     occ_load.start()
     for k in range(n_small):
         small_load(k).start()
-    for k in range(n_whole):
-        whole_load(k).start()
 
     barrier = pltpu.get_barrier_semaphore()
 
@@ -157,10 +162,12 @@
 
     def t_send(is_small, k):
         for r in ORDER:
-            t_copy(is_small, k, peer_orb(r), me).start()
+            t_copy(is_small, k, peer_at(r), me).start()
 
     def t_small():
         small_load(0).wait()
+        for k in range(n_whole):
+            whole_load(k).start()
 
         def step(j, carry):
             t_part(SMALL_STEP, whole + j * SMALL_STEP, j * SMALL_STEP, rest, True)
@@ -208,7 +215,7 @@
         gsend[...] = total
         grecv[me] = total
         for r in ORDER:
-            g_copy(peer_orb(r), me).start()
+            g_copy(peer_at(r), me).start()
 
     def coulomb():
         for r in range(1, n_orb):
@@ -277,9 +284,9 @@
     t_small()
     lax.fori_loop(0, n_whole, t_whole, 0)
     for r in ORDER:
-        l_copy(0, peer_orb(r), me).start()
+        l_copy(0, peer_at(r), me).start()
     for r in ORDER:
-        if_last(peer_orb(r), l_copy(1, peer_orb(r), me).start)
+        if_last(peer_at(r), l_copy(1, peer_at(r), me).start)
     ex_recv[me] = ex_send[me]
     xa[...] = jnp.zeros(xa.shape, jnp.float32)
     coulomb()
@@ -317,10 +324,11 @@
     def hops(step, ring):
         return min(step, ring - step)
 
-    steps = sorted(range(1, n_dev), key=lambda k: -(hops((k % n_orb + 1) // 2, n_orb // 2) + hops(k // n_orb, n_aux)))
+    steps = [(ahead, flip, up) for ahead in range(n_chips) for flip in range(2) for up in range(n_aux)][1:]
+    steps = sorted(steps, key=lambda p: -(hops(p[0], n_chips) + hops(p[2], n_aux)))
 
     def k_out(step):
-        return k_copy(peer_orb(step % n_orb), lax.rem(my + step // n_orb, n_aux), dev)
+        return k_copy(peer_at(step[:2]), lax.rem(my + step[2], n_aux), dev)
 
     for step in steps:
         k_out(step).start()
@@ -340,7 +348,7 @@
         jsum = jsum + jrecv[src]
 
     for step in reversed(steps):
-        k_copy(me, my, lax.rem(my + step // n_orb, n_aux) * n_orb + peer_orb(step % n_orb)).wait_recv()
+        k_copy(me, my, lax.rem(my + step[2], n_aux) * n_orb + peer_at(step[:2])).wait_recv()
     ksum = krecv[0]
     for src in range(1, n_dev):
         ksum = ksum + krecv[src]
@@ -379,7 +387,7 @@
         dims = (n_orb, n_aux, q_loc, row_blk, n_bf, n_occ, row_pad, occ_each, q_main, left_pad, fold, n_cols)
         n_dev = n_orb * n_aux
         n_groups = 1 + whole // SUBL
-        assert rest % SMALL_STEP == 0 and slots * rest % SUBL == 0 and slots % 2 == 0 and pairs == 2
+        assert len(ORDER) == n_orb - 1 and rest % SMALL_STEP == 0 and slots * rest % SUBL == 0 and slots % 2 == 0 and pairs == 2
         ex_rows = rup(pairs * row_blk, SUBL) + rup(row_blk, SUBL)
         q_lanes = rup(q_loc, LANES)
         g_rows = rup(q_lanes // LANES, 4)

time: 39.9 us -> 39.5 us (0.990)
  Pallas kernels: 39.2 us -> 38.8 us
where the time goes in v6:
time: 39.5 us; the launch traced here: 39.4 us
  Pallas kernels  38.8 us (98%)
  local copies, waits for them, and re-layouts  0.61 us (2%)
    pallas_call x1, Pallas kernels, local_fock(): pl.pallas_call(functools.partial(fock_kernel, dims), out_shape=jax.ShapeD...  38.8 us

profile of v6, /device:TPU:97, one launch (start us, length us, event | category | flops | bytes accessed | tf_op | source)
XLA Modules:
  0.0 39.4 jit_solution(12135576008378418551)
XLA Ops:
  0.0 38.8 %fock_build.1 = f32[30,60]{1,0:T(8,128)S(1)} custom-call(f32[30,290,240]{2,1,0:T(8,128)} %bitcast.2, f32[50,240]{1,0:T(8,128)} %bitcast.3), custom_call_target="tpu_custom_call" | custom-call | tf_op jit(solution)/shard_map/fock_build/pallas_call | solution.py:419
  38.8 0.6 %copy.4 = f32[30,60]{1,0:T(8,128)} copy(f32[30,60]{1,0:T(8,128)S(1)} %fock_build.1) | data formatting | bytes 14400

commit v7 on v6

--- a/solution.py
+++ b/solution.py
@@ -64,17 +64,17 @@
     def whole_load(k):
         return load(k * SUBL, SUBL, n_small + k)
 
+    barrier = pltpu.get_barrier_semaphore()
+
+    for r in ORDER:
+        pl.semaphore_signal(barrier, inc=1, device_id={'orb': peer_at(r)}, device_id_type=MESH_ID)
+    for r in range(1, n_aux):
+        pl.semaphore_signal(barrier, inc=1, device_id={'aux': lax.rem(my + r, n_aux)}, device_id_type=MESH_ID)
     occ_load = pltpu.make_async_copy(occ_ref, ct, load_sem.at[n_groups])
     occ_load.start()
     for k in range(n_small):
         small_load(k).start()
 
-    barrier = pltpu.get_barrier_semaphore()
-
-    for r in range(1, n_orb):
-        pl.semaphore_signal(barrier, inc=1, device_id={'orb': peer_orb(r)}, device_id_type=MESH_ID)
-    for r in range(1, n_aux):
-        pl.semaphore_signal(barrier, inc=1, device_id={'aux': lax.rem(my + r, n_aux)}, device_id_type=MESH_ID)
     ex_send[...] = jnp.zeros(ex_send.shape, jnp.float32)
 
     occ_load.wait()

time: 39.5 us -> 39.5 us (level)
  no operation moved by 1% of the time
where the time goes in v7:
time: 39.5 us; the launch traced here: 39.4 us
  Pallas kernels  38.8 us (98%)
  local copies, waits for them, and re-layouts  0.61 us (2%)
    pallas_call x1, Pallas kernels, local_fock(): pl.pallas_call(functools.partial(fock_kernel, dims), out_shape=jax.ShapeD...  38.8 us

profile of v7, /device:TPU:97, one launch (start us, length us, event | category | flops | bytes accessed | tf_op | source)
XLA Modules:
  0.0 39.4 jit_solution(14106492028812765084)
XLA Ops:
  0.0 38.8 %fock_build.1 = f32[30,60]{1,0:T(8,128)S(1)} custom-call(f32[30,290,240]{2,1,0:T(8,128)} %bitcast.2, f32[50,240]{1,0:T(8,128)} %bitcast.3), custom_call_target="tpu_custom_call" | custom-call | tf_op jit(solution)/shard_map/fock_build/pallas_call | solution.py:419
  38.8 0.6 %copy.4 = f32[30,60]{1,0:T(8,128)} copy(f32[30,60]{1,0:T(8,128)S(1)} %fock_build.1) | data formatting | bytes 14400
